TPU v7x, 32 devices: a 4x4x1 block of a 4x4x8 slice. The times are simulated.
32 devices in a mesh: task: 1 (over z), row: 32 (over y, x, core).
Axes of the slice: x: 4, y: 4, z: 1, core: 2. Of those that a mesh axis runs over, the one named last changes fastest.
The devices are a block of a 4x4x8 slice.
Arguments:
- points: bfloat16 [49152, 128], P(('task', 'row'))
- vectors: bfloat16 [49152, 16], P(('task', 'row'))
- length_scale: float32 [1], P('task')
- out_scale: float32 [1], P('task')
Outputs:
- output: float32 [49152, 16], P(('task', 'row'))
All inputs are finite; a program needn't handle non-finite values.
Results may differ from a plain program's by a relative error of at most 0.001.
Values are sent between devices in bfloat16 or wider.
A program may use at most 768 MiB of HBM per device.

v0:
```python
import jax
import jax.numpy as jnp
from jax import lax
from jax.sharding import PartitionSpec as P


def solution(mesh):
    n_row = mesh.shape["row"]
    shift_pairs = [(source_idx, (source_idx + 1) % n_row) for source_idx in range(n_row)]

    def kernel_product(x_rows, norm_rows, x_cols, norm_cols, v_cols, length_scale, out_scale):
        gram_mat = jnp.einsum("if,jf->ij", x_rows, x_cols, preferred_element_type=jnp.float32)
        sq_dist = jnp.maximum(norm_rows[:, None] + norm_cols[None, :] - 2.0 * gram_mat, 0.0)
        kern_tile = (out_scale * jnp.exp(-sq_dist / (2.0 * length_scale * length_scale))).astype(jnp.bfloat16)
        return jnp.dot(kern_tile, v_cols, preferred_element_type=jnp.float32)

    def kernel_pass(x_loc, norm_loc, v_loc, length_scale, out_scale):
        own_part = kernel_product(x_loc, norm_loc, x_loc, norm_loc, v_loc, length_scale, out_scale)

        def visit_step(step_idx, loop_state):
            x_vis, v_vis, running = loop_state
            x_vis = lax.ppermute(x_vis, "row", shift_pairs)
            v_vis = lax.ppermute(v_vis, "row", shift_pairs)
            norm_vis = jnp.sum(jnp.square(x_vis.astype(jnp.float32)), axis=1)
            running = running + kernel_product(x_loc, norm_loc, x_vis, norm_vis, v_vis, length_scale, out_scale)
            return x_vis, v_vis, running

        final_state = lax.fori_loop(1, n_row, visit_step, (x_loc, v_loc, own_part))
        return final_state[2]

    def local_program(x_loc, v_loc, length_scale, out_scale):
        norm_loc = jnp.sum(jnp.square(x_loc.astype(jnp.float32)), axis=1)
        first_pass = kernel_pass(x_loc, norm_loc, v_loc, length_scale, out_scale).astype(jnp.bfloat16)
        return kernel_pass(x_loc, norm_loc, first_pass, length_scale, out_scale)

    row_spec = P(("task", "row"), None)
    return jax.shard_map(local_program, mesh=mesh, in_specs=(row_spec, row_spec, P("task"), P("task")), out_specs=row_spec, check_vma=False)
```

profile of v0, /device:TPU:97, one launch (start us, length us, event | category | flops | bytes accessed | tf_op | source)
XLA Modules:
  0.0 984.0 jit_solution(11594714262613837621)
XLA Ops:
  11.1 481.0 %while.32 = (s32[]{:T(128)}, bf16[1536,128]{1,0:T(8,128)(2,1)S(1)}, bf16[1536,16]{0,1:T(8,128)(2,1)S(1)}, f32[1536,16]{0,1:T(8,128)S(1)}, f32[1]{0:T(128)}, /*in...) while((s32[]{:T(128)}, bf16[1536,128]{1,0:T(8,128)(2,1)S(1)}, ...), condition=%wide.region_3.0_spmd, body=%wide.region_1.0_spmd.sunk | while | flops 698964480 | bytes 4098229 | solution.py:28
  52.1 10.9 %collective-permute-done.1 = bf16[1536,16]{0,1:T(8,128)(2,1)S(1)} collective-permute-done((bf16[1536,16]{0,1:T(8,128)(2,1)S(1)}, bf16[1536,16]{0,1:T(8,128)(2,1)S(1)}, u32[]{:S(2)}, u32[]{:S(2)}) %collective-permute-start.1) | collective-permute-done | bytes 49184 | tf_op jit(solution)/shard_map/while/body/eval_jaxpr/ppermute | solution.py:23
  67.8 10.9 %collective-permute-done.1 = bf16[1536,16]{0,1:T(8,128)(2,1)S(1)} collective-permute-done((bf16[1536,16]{0,1:T(8,128)(2,1)S(1)}, bf16[1536,16]{0,1:T(8,128)(2,1)S(1)}, u32[]{:S(2)}, u32[]{:S(2)}) %collective-permute-start.1) | collective-permute-done | bytes 49184 | tf_op jit(solution)/shard_map/while/body/eval_jaxpr/ppermute | solution.py:23
  83.5 10.9 %collective-permute-done.1 = bf16[1536,16]{0,1:T(8,128)(2,1)S(1)} collective-permute-done((bf16[1536,16]{0,1:T(8,128)(2,1)S(1)}, bf16[1536,16]{0,1:T(8,128)(2,1)S(1)}, u32[]{:S(2)}, u32[]{:S(2)}) %collective-permute-start.1) | collective-permute-done | bytes 49184 | tf_op jit(solution)/shard_map/while/body/eval_jaxpr/ppermute | solution.py:23
  99.3 10.9 %collective-permute-done.1 = bf16[1536,16]{0,1:T(8,128)(2,1)S(1)} collective-permute-done((bf16[1536,16]{0,1:T(8,128)(2,1)S(1)}, bf16[1536,16]{0,1:T(8,128)(2,1)S(1)}, u32[]{:S(2)}, u32[]{:S(2)}) %collective-permute-start.1) | collective-permute-done | bytes 49184 | tf_op jit(solution)/shard_map/while/body/eval_jaxpr/ppermute | solution.py:23
  115.0 10.9 %collective-permute-done.1 = bf16[1536,16]{0,1:T(8,128)(2,1)S(1)} collective-permute-done((bf16[1536,16]{0,1:T(8,128)(2,1)S(1)}, bf16[1536,16]{0,1:T(8,128)(2,1)S(1)}, u32[]{:S(2)}, u32[]{:S(2)}) %collective-permute-start.1) | collective-permute-done | bytes 49184 | tf_op jit(solution)/shard_map/while/body/eval_jaxpr/ppermute | solution.py:23
  130.7 10.9 %collective-permute-done.1 = bf16[1536,16]{0,1:T(8,128)(2,1)S(1)} collective-permute-done((bf16[1536,16]{0,1:T(8,128)(2,1)S(1)}, bf16[1536,16]{0,1:T(8,128)(2,1)S(1)}, u32[]{:S(2)}, u32[]{:S(2)}) %collective-permute-start.1) | collective-permute-done | bytes 49184 | tf_op jit(solution)/shard_map/while/body/eval_jaxpr/ppermute | solution.py:23
  146.4 10.9 %collective-permute-done.1 = bf16[1536,16]{0,1:T(8,128)(2,1)S(1)} collective-permute-done((bf16[1536,16]{0,1:T(8,128)(2,1)S(1)}, bf16[1536,16]{0,1:T(8,128)(2,1)S(1)}, u32[]{:S(2)}, u32[]{:S(2)}) %collective-permute-start.1) | collective-permute-done | bytes 49184 | tf_op jit(solution)/shard_map/while/body/eval_jaxpr/ppermute | solution.py:23
  162.2 10.9 %collective-permute-done.1 = bf16[1536,16]{0,1:T(8,128)(2,1)S(1)} collective-permute-done((bf16[1536,16]{0,1:T(8,128)(2,1)S(1)}, bf16[1536,16]{0,1:T(8,128)(2,1)S(1)}, u32[]{:S(2)}, u32[]{:S(2)}) %collective-permute-start.1) | collective-permute-done | bytes 49184 | tf_op jit(solution)/shard_map/while/body/eval_jaxpr/ppermute | solution.py:23
  177.9 10.9 %collective-permute-done.1 = bf16[1536,16]{0,1:T(8,128)(2,1)S(1)} collective-permute-done((bf16[1536,16]{0,1:T(8,128)(2,1)S(1)}, bf16[1536,16]{0,1:T(8,128)(2,1)S(1)}, u32[]{:S(2)}, u32[]{:S(2)}) %collective-permute-start.1) | collective-permute-done | bytes 49184 | tf_op jit(solution)/shard_map/while/body/eval_jaxpr/ppermute | solution.py:23
  193.6 10.9 %collective-permute-done.1 = bf16[1536,16]{0,1:T(8,128)(2,1)S(1)} collective-permute-done((bf16[1536,16]{0,1:T(8,128)(2,1)S(1)}, bf16[1536,16]{0,1:T(8,128)(2,1)S(1)}, u32[]{:S(2)}, u32[]{:S(2)}) %collective-permute-start.1) | collective-permute-done | bytes 49184 | tf_op jit(solution)/shard_map/while/body/eval_jaxpr/ppermute | solution.py:23
  209.3 10.9 %collective-permute-done.1 = bf16[1536,16]{0,1:T(8,128)(2,1)S(1)} collective-permute-done((bf16[1536,16]{0,1:T(8,128)(2,1)S(1)}, bf16[1536,16]{0,1:T(8,128)(2,1)S(1)}, u32[]{:S(2)}, u32[]{:S(2)}) %collective-permute-start.1) | collective-permute-done | bytes 49184 | tf_op jit(solution)/shard_map/while/body/eval_jaxpr/ppermute | solution.py:23
  225.0 10.9 %collective-permute-done.1 = bf16[1536,16]{0,1:T(8,128)(2,1)S(1)} collective-permute-done((bf16[1536,16]{0,1:T(8,128)(2,1)S(1)}, bf16[1536,16]{0,1:T(8,128)(2,1)S(1)}, u32[]{:S(2)}, u32[]{:S(2)}) %collective-permute-start.1) | collective-permute-done | bytes 49184 | tf_op jit(solution)/shard_map/while/body/eval_jaxpr/ppermute | solution.py:23
  240.8 10.9 %collective-permute-done.1 = bf16[1536,16]{0,1:T(8,128)(2,1)S(1)} collective-permute-done((bf16[1536,16]{0,1:T(8,128)(2,1)S(1)}, bf16[1536,16]{0,1:T(8,128)(2,1)S(1)}, u32[]{:S(2)}, u32[]{:S(2)}) %collective-permute-start.1) | collective-permute-done | bytes 49184 | tf_op jit(solution)/shard_map/while/body/eval_jaxpr/ppermute | solution.py:23
  256.5 10.9 %collective-permute-done.1 = bf16[1536,16]{0,1:T(8,128)(2,1)S(1)} collective-permute-done((bf16[1536,16]{0,1:T(8,128)(2,1)S(1)}, bf16[1536,16]{0,1:T(8,128)(2,1)S(1)}, u32[]{:S(2)}, u32[]{:S(2)}) %collective-permute-start.1) | collective-permute-done | bytes 49184 | tf_op jit(solution)/shard_map/while/body/eval_jaxpr/ppermute | solution.py:23
  272.2 10.9 %collective-permute-done.1 = bf16[1536,16]{0,1:T(8,128)(2,1)S(1)} collective-permute-done((bf16[1536,16]{0,1:T(8,128)(2,1)S(1)}, bf16[1536,16]{0,1:T(8,128)(2,1)S(1)}, u32[]{:S(2)}, u32[]{:S(2)}) %collective-permute-start.1) | collective-permute-done | bytes 49184 | tf_op jit(solution)/shard_map/while/body/eval_jaxpr/ppermute | solution.py:23
  287.9 10.9 %collective-permute-done.1 = bf16[1536,16]{0,1:T(8,128)(2,1)S(1)} collective-permute-done((bf16[1536,16]{0,1:T(8,128)(2,1)S(1)}, bf16[1536,16]{0,1:T(8,128)(2,1)S(1)}, u32[]{:S(2)}, u32[]{:S(2)}) %collective-permute-start.1) | collective-permute-done | bytes 49184 | tf_op jit(solution)/shard_map/while/body/eval_jaxpr/ppermute | solution.py:23
  303.7 10.9 %collective-permute-done.1 = bf16[1536,16]{0,1:T(8,128)(2,1)S(1)} collective-permute-done((bf16[1536,16]{0,1:T(8,128)(2,1)S(1)}, bf16[1536,16]{0,1:T(8,128)(2,1)S(1)}, u32[]{:S(2)}, u32[]{:S(2)}) %collective-permute-start.1) | collective-permute-done | bytes 49184 | tf_op jit(solution)/shard_map/while/body/eval_jaxpr/ppermute | solution.py:23
  319.4 10.9 %collective-permute-done.1 = bf16[1536,16]{0,1:T(8,128)(2,1)S(1)} collective-permute-done((bf16[1536,16]{0,1:T(8,128)(2,1)S(1)}, bf16[1536,16]{0,1:T(8,128)(2,1)S(1)}, u32[]{:S(2)}, u32[]{:S(2)}) %collective-permute-start.1) | collective-permute-done | bytes 49184 | tf_op jit(solution)/shard_map/while/body/eval_jaxpr/ppermute | solution.py:23
  335.1 10.9 %collective-permute-done.1 = bf16[1536,16]{0,1:T(8,128)(2,1)S(1)} collective-permute-done((bf16[1536,16]{0,1:T(8,128)(2,1)S(1)}, bf16[1536,16]{0,1:T(8,128)(2,1)S(1)}, u32[]{:S(2)}, u32[]{:S(2)}) %collective-permute-start.1) | collective-permute-done | bytes 49184 | tf_op jit(solution)/shard_map/while/body/eval_jaxpr/ppermute | solution.py:23
  350.8 10.9 %collective-permute-done.1 = bf16[1536,16]{0,1:T(8,128)(2,1)S(1)} collective-permute-done((bf16[1536,16]{0,1:T(8,128)(2,1)S(1)}, bf16[1536,16]{0,1:T(8,128)(2,1)S(1)}, u32[]{:S(2)}, u32[]{:S(2)}) %collective-permute-start.1) | collective-permute-done | bytes 49184 | tf_op jit(solution)/shard_map/while/body/eval_jaxpr/ppermute | solution.py:23
  366.5 10.9 %collective-permute-done.1 = bf16[1536,16]{0,1:T(8,128)(2,1)S(1)} collective-permute-done((bf16[1536,16]{0,1:T(8,128)(2,1)S(1)}, bf16[1536,16]{0,1:T(8,128)(2,1)S(1)}, u32[]{:S(2)}, u32[]{:S(2)}) %collective-permute-start.1) | collective-permute-done | bytes 49184 | tf_op jit(solution)/shard_map/while/body/eval_jaxpr/ppermute | solution.py:23
  382.3 10.9 %collective-permute-done.1 = bf16[1536,16]{0,1:T(8,128)(2,1)S(1)} collective-permute-done((bf16[1536,16]{0,1:T(8,128)(2,1)S(1)}, bf16[1536,16]{0,1:T(8,128)(2,1)S(1)}, u32[]{:S(2)}, u32[]{:S(2)}) %collective-permute-start.1) | collective-permute-done | bytes 49184 | tf_op jit(solution)/shard_map/while/body/eval_jaxpr/ppermute | solution.py:23
  398.0 10.9 %collective-permute-done.1 = bf16[1536,16]{0,1:T(8,128)(2,1)S(1)} collective-permute-done((bf16[1536,16]{0,1:T(8,128)(2,1)S(1)}, bf16[1536,16]{0,1:T(8,128)(2,1)S(1)}, u32[]{:S(2)}, u32[]{:S(2)}) %collective-permute-start.1) | collective-permute-done | bytes 49184 | tf_op jit(solution)/shard_map/while/body/eval_jaxpr/ppermute | solution.py:23
  413.7 10.9 %collective-permute-done.1 = bf16[1536,16]{0,1:T(8,128)(2,1)S(1)} collective-permute-done((bf16[1536,16]{0,1:T(8,128)(2,1)S(1)}, bf16[1536,16]{0,1:T(8,128)(2,1)S(1)}, u32[]{:S(2)}, u32[]{:S(2)}) %collective-permute-start.1) | collective-permute-done | bytes 49184 | tf_op jit(solution)/shard_map/while/body/eval_jaxpr/ppermute | solution.py:23
  429.4 10.9 %collective-permute-done.1 = bf16[1536,16]{0,1:T(8,128)(2,1)S(1)} collective-permute-done((bf16[1536,16]{0,1:T(8,128)(2,1)S(1)}, bf16[1536,16]{0,1:T(8,128)(2,1)S(1)}, u32[]{:S(2)}, u32[]{:S(2)}) %collective-permute-start.1) | collective-permute-done | bytes 49184 | tf_op jit(solution)/shard_map/while/body/eval_jaxpr/ppermute | solution.py:23
  445.1 10.9 %collective-permute-done.1 = bf16[1536,16]{0,1:T(8,128)(2,1)S(1)} collective-permute-done((bf16[1536,16]{0,1:T(8,128)(2,1)S(1)}, bf16[1536,16]{0,1:T(8,128)(2,1)S(1)}, u32[]{:S(2)}, u32[]{:S(2)}) %collective-permute-start.1) | collective-permute-done | bytes 49184 | tf_op jit(solution)/shard_map/while/body/eval_jaxpr/ppermute | solution.py:23
  460.9 10.9 %collective-permute-done.1 = bf16[1536,16]{0,1:T(8,128)(2,1)S(1)} collective-permute-done((bf16[1536,16]{0,1:T(8,128)(2,1)S(1)}, bf16[1536,16]{0,1:T(8,128)(2,1)S(1)}, u32[]{:S(2)}, u32[]{:S(2)}) %collective-permute-start.1) | collective-permute-done | bytes 49184 | tf_op jit(solution)/shard_map/while/body/eval_jaxpr/ppermute | solution.py:23
  476.6 10.9 %collective-permute-done.1 = bf16[1536,16]{0,1:T(8,128)(2,1)S(1)} collective-permute-done((bf16[1536,16]{0,1:T(8,128)(2,1)S(1)}, bf16[1536,16]{0,1:T(8,128)(2,1)S(1)}, u32[]{:S(2)}, u32[]{:S(2)}) %collective-permute-start.1) | collective-permute-done | bytes 49184 | tf_op jit(solution)/shard_map/while/body/eval_jaxpr/ppermute | solution.py:23
  495.9 487.5 %while.33 = (s32[]{:T(128)}, bf16[1536,128]{1,0:T(8,128)(2,1)S(1)}, bf16[1536,16]{0,1:T(8,128)(2,1)S(1)}, f32[1536,16]{0,1:T(8,128)S(1)}, f32[1]{0:T(128)}, /*in...) while((s32[]{:T(128)}, bf16[1536,128]{1,0:T(8,128)(2,1)S(1)}, ...), condition=%wide.region_6.0_spmd, body=%wide.region_4.0_spmd.sunk | while | flops 698964480 | bytes 4098229 | solution.py:28
  496.1 10.9 %collective-permute-done.3 = bf16[1536,16]{0,1:T(8,128)(2,1)S(1)} collective-permute-done((bf16[1536,16]{0,1:T(8,128)(2,1)S(1)}, bf16[1536,16]{0,1:T(8,128)(2,1)S(1)}, u32[]{:S(2)}, u32[]{:S(2)}) %collective-permute-start.3) | collective-permute-done | bytes 49184 | tf_op jit(solution)/shard_map/while/body/eval_jaxpr/ppermute | solution.py:23
  527.6 10.9 %collective-permute-done.3 = bf16[1536,16]{0,1:T(8,128)(2,1)S(1)} collective-permute-done((bf16[1536,16]{0,1:T(8,128)(2,1)S(1)}, bf16[1536,16]{0,1:T(8,128)(2,1)S(1)}, u32[]{:S(2)}, u32[]{:S(2)}) %collective-permute-start.3) | collective-permute-done | bytes 49184 | tf_op jit(solution)/shard_map/while/body/eval_jaxpr/ppermute | solution.py:23
  543.3 10.9 %collective-permute-done.3 = bf16[1536,16]{0,1:T(8,128)(2,1)S(1)} collective-permute-done((bf16[1536,16]{0,1:T(8,128)(2,1)S(1)}, bf16[1536,16]{0,1:T(8,128)(2,1)S(1)}, u32[]{:S(2)}, u32[]{:S(2)}) %collective-permute-start.3) | collective-permute-done | bytes 49184 | tf_op jit(solution)/shard_map/while/body/eval_jaxpr/ppermute | solution.py:23
  559.0 10.9 %collective-permute-done.3 = bf16[1536,16]{0,1:T(8,128)(2,1)S(1)} collective-permute-done((bf16[1536,16]{0,1:T(8,128)(2,1)S(1)}, bf16[1536,16]{0,1:T(8,128)(2,1)S(1)}, u32[]{:S(2)}, u32[]{:S(2)}) %collective-permute-start.3) | collective-permute-done | bytes 49184 | tf_op jit(solution)/shard_map/while/body/eval_jaxpr/ppermute | solution.py:23
  574.7 10.9 %collective-permute-done.3 = bf16[1536,16]{0,1:T(8,128)(2,1)S(1)} collective-permute-done((bf16[1536,16]{0,1:T(8,128)(2,1)S(1)}, bf16[1536,16]{0,1:T(8,128)(2,1)S(1)}, u32[]{:S(2)}, u32[]{:S(2)}) %collective-permute-start.3) | collective-permute-done | bytes 49184 | tf_op jit(solution)/shard_map/while/body/eval_jaxpr/ppermute | solution.py:23
  590.5 10.9 %collective-permute-done.3 = bf16[1536,16]{0,1:T(8,128)(2,1)S(1)} collective-permute-done((bf16[1536,16]{0,1:T(8,128)(2,1)S(1)}, bf16[1536,16]{0,1:T(8,128)(2,1)S(1)}, u32[]{:S(2)}, u32[]{:S(2)}) %collective-permute-start.3) | collective-permute-done | bytes 49184 | tf_op jit(solution)/shard_map/while/body/eval_jaxpr/ppermute | solution.py:23
  606.2 10.9 %collective-permute-done.3 = bf16[1536,16]{0,1:T(8,128)(2,1)S(1)} collective-permute-done((bf16[1536,16]{0,1:T(8,128)(2,1)S(1)}, bf16[1536,16]{0,1:T(8,128)(2,1)S(1)}, u32[]{:S(2)}, u32[]{:S(2)}) %collective-permute-start.3) | collective-permute-done | bytes 49184 | tf_op jit(solution)/shard_map/while/body/eval_jaxpr/ppermute | solution.py:23
  621.9 10.9 %collective-permute-done.3 = bf16[1536,16]{0,1:T(8,128)(2,1)S(1)} collective-permute-done((bf16[1536,16]{0,1:T(8,128)(2,1)S(1)}, bf16[1536,16]{0,1:T(8,128)(2,1)S(1)}, u32[]{:S(2)}, u32[]{:S(2)}) %collective-permute-start.3) | collective-permute-done | bytes 49184 | tf_op jit(solution)/shard_map/while/body/eval_jaxpr/ppermute | solution.py:23
  637.6 10.9 %collective-permute-done.3 = bf16[1536,16]{0,1:T(8,128)(2,1)S(1)} collective-permute-done((bf16[1536,16]{0,1:T(8,128)(2,1)S(1)}, bf16[1536,16]{0,1:T(8,128)(2,1)S(1)}, u32[]{:S(2)}, u32[]{:S(2)}) %collective-permute-start.3) | collective-permute-done | bytes 49184 | tf_op jit(solution)/shard_map/while/body/eval_jaxpr/ppermute | solution.py:23
  653.4 10.9 %collective-permute-done.3 = bf16[1536,16]{0,1:T(8,128)(2,1)S(1)} collective-permute-done((bf16[1536,16]{0,1:T(8,128)(2,1)S(1)}, bf16[1536,16]{0,1:T(8,128)(2,1)S(1)}, u32[]{:S(2)}, u32[]{:S(2)}) %collective-permute-start.3) | collective-permute-done | bytes 49184 | tf_op jit(solution)/shard_map/while/body/eval_jaxpr/ppermute | solution.py:23
  669.1 10.9 %collective-permute-done.3 = bf16[1536,16]{0,1:T(8,128)(2,1)S(1)} collective-permute-done((bf16[1536,16]{0,1:T(8,128)(2,1)S(1)}, bf16[1536,16]{0,1:T(8,128)(2,1)S(1)}, u32[]{:S(2)}, u32[]{:S(2)}) %collective-permute-start.3) | collective-permute-done | bytes 49184 | tf_op jit(solution)/shard_map/while/body/eval_jaxpr/ppermute | solution.py:23
  684.8 10.9 %collective-permute-done.3 = bf16[1536,16]{0,1:T(8,128)(2,1)S(1)} collective-permute-done((bf16[1536,16]{0,1:T(8,128)(2,1)S(1)}, bf16[1536,16]{0,1:T(8,128)(2,1)S(1)}, u32[]{:S(2)}, u32[]{:S(2)}) %collective-permute-start.3) | collective-permute-done | bytes 49184 | tf_op jit(solution)/shard_map/while/body/eval_jaxpr/ppermute | solution.py:23
  700.5 10.9 %collective-permute-done.3 = bf16[1536,16]{0,1:T(8,128)(2,1)S(1)} collective-permute-done((bf16[1536,16]{0,1:T(8,128)(2,1)S(1)}, bf16[1536,16]{0,1:T(8,128)(2,1)S(1)}, u32[]{:S(2)}, u32[]{:S(2)}) %collective-permute-start.3) | collective-permute-done | bytes 49184 | tf_op jit(solution)/shard_map/while/body/eval_jaxpr/ppermute | solution.py:23
  716.2 10.9 %collective-permute-done.3 = bf16[1536,16]{0,1:T(8,128)(2,1)S(1)} collective-permute-done((bf16[1536,16]{0,1:T(8,128)(2,1)S(1)}, bf16[1536,16]{0,1:T(8,128)(2,1)S(1)}, u32[]{:S(2)}, u32[]{:S(2)}) %collective-permute-start.3) | collective-permute-done | bytes 49184 | tf_op jit(solution)/shard_map/while/body/eval_jaxpr/ppermute | solution.py:23
  732.0 10.9 %collective-permute-done.3 = bf16[1536,16]{0,1:T(8,128)(2,1)S(1)} collective-permute-done((bf16[1536,16]{0,1:T(8,128)(2,1)S(1)}, bf16[1536,16]{0,1:T(8,128)(2,1)S(1)}, u32[]{:S(2)}, u32[]{:S(2)}) %collective-permute-start.3) | collective-permute-done | bytes 49184 | tf_op jit(solution)/shard_map/while/body/eval_jaxpr/ppermute | solution.py:23
  747.7 10.9 %collective-permute-done.3 = bf16[1536,16]{0,1:T(8,128)(2,1)S(1)} collective-permute-done((bf16[1536,16]{0,1:T(8,128)(2,1)S(1)}, bf16[1536,16]{0,1:T(8,128)(2,1)S(1)}, u32[]{:S(2)}, u32[]{:S(2)}) %collective-permute-start.3) | collective-permute-done | bytes 49184 | tf_op jit(solution)/shard_map/while/body/eval_jaxpr/ppermute | solution.py:23
  794.9 10.9 %collective-permute-done.3 = bf16[1536,16]{0,1:T(8,128)(2,1)S(1)} collective-permute-done((bf16[1536,16]{0,1:T(8,128)(2,1)S(1)}, bf16[1536,16]{0,1:T(8,128)(2,1)S(1)}, u32[]{:S(2)}, u32[]{:S(2)}) %collective-permute-start.3) | collective-permute-done | bytes 49184 | tf_op jit(solution)/shard_map/while/body/eval_jaxpr/ppermute | solution.py:23
  857.7 10.9 %collective-permute-done.3 = bf16[1536,16]{0,1:T(8,128)(2,1)S(1)} collective-permute-done((bf16[1536,16]{0,1:T(8,128)(2,1)S(1)}, bf16[1536,16]{0,1:T(8,128)(2,1)S(1)}, u32[]{:S(2)}, u32[]{:S(2)}) %collective-permute-start.3) | collective-permute-done | bytes 49184 | tf_op jit(solution)/shard_map/while/body/eval_jaxpr/ppermute | solution.py:23
  (464 shorter events, 478.2 us)
Async XLA Ops:
  52.0 11.1 %collective-permute-start = (bf16[1536,128]{1,0:T(8,128)(2,1)S(1)}, bf16[1536,128]{1,0:T(8,128)(2,1)S(1)}, u32[]{:S(2)}, u32[]{:S(2)}) collective-permute-start(bf16[1536,128]{1,0:T(8,128)(2,1)S(1)} %get-tuple-element.337), channel_id=1, source_target_pairs={{0,1},{1,2},{2,3},{3,4},{4,5},{5,6},{6,7},{7,8},{8,9},{9,10},{10,1... | collective-permute-start | bytes 1179656 | tf_op jit(solution)/shard_map/while/body/eval_jaxpr/ppermute | solution.py:22
  67.7 11.1 %collective-permute-start = (bf16[1536,128]{1,0:T(8,128)(2,1)S(1)}, bf16[1536,128]{1,0:T(8,128)(2,1)S(1)}, u32[]{:S(2)}, u32[]{:S(2)}) collective-permute-start(bf16[1536,128]{1,0:T(8,128)(2,1)S(1)} %get-tuple-element.337), channel_id=1, source_target_pairs={{0,1},{1,2},{2,3},{3,4},{4,5},{5,6},{6,7},{7,8},{8,9},{9,10},{10,1... | collective-permute-start | bytes 1179656 | tf_op jit(solution)/shard_map/while/body/eval_jaxpr/ppermute | solution.py:22
  83.4 11.1 %collective-permute-start = (bf16[1536,128]{1,0:T(8,128)(2,1)S(1)}, bf16[1536,128]{1,0:T(8,128)(2,1)S(1)}, u32[]{:S(2)}, u32[]{:S(2)}) collective-permute-start(bf16[1536,128]{1,0:T(8,128)(2,1)S(1)} %get-tuple-element.337), channel_id=1, source_target_pairs={{0,1},{1,2},{2,3},{3,4},{4,5},{5,6},{6,7},{7,8},{8,9},{9,10},{10,1... | collective-permute-start | bytes 1179656 | tf_op jit(solution)/shard_map/while/body/eval_jaxpr/ppermute | solution.py:22
  99.1 11.1 %collective-permute-start = (bf16[1536,128]{1,0:T(8,128)(2,1)S(1)}, bf16[1536,128]{1,0:T(8,128)(2,1)S(1)}, u32[]{:S(2)}, u32[]{:S(2)}) collective-permute-start(bf16[1536,128]{1,0:T(8,128)(2,1)S(1)} %get-tuple-element.337), channel_id=1, source_target_pairs={{0,1},{1,2},{2,3},{3,4},{4,5},{5,6},{6,7},{7,8},{8,9},{9,10},{10,1... | collective-permute-start | bytes 1179656 | tf_op jit(solution)/shard_map/while/body/eval_jaxpr/ppermute | solution.py:22
  114.8 11.1 %collective-permute-start = (bf16[1536,128]{1,0:T(8,128)(2,1)S(1)}, bf16[1536,128]{1,0:T(8,128)(2,1)S(1)}, u32[]{:S(2)}, u32[]{:S(2)}) collective-permute-start(bf16[1536,128]{1,0:T(8,128)(2,1)S(1)} %get-tuple-element.337), channel_id=1, source_target_pairs={{0,1},{1,2},{2,3},{3,4},{4,5},{5,6},{6,7},{7,8},{8,9},{9,10},{10,1... | collective-permute-start | bytes 1179656 | tf_op jit(solution)/shard_map/while/body/eval_jaxpr/ppermute | solution.py:22
  130.6 11.1 %collective-permute-start = (bf16[1536,128]{1,0:T(8,128)(2,1)S(1)}, bf16[1536,128]{1,0:T(8,128)(2,1)S(1)}, u32[]{:S(2)}, u32[]{:S(2)}) collective-permute-start(bf16[1536,128]{1,0:T(8,128)(2,1)S(1)} %get-tuple-element.337), channel_id=1, source_target_pairs={{0,1},{1,2},{2,3},{3,4},{4,5},{5,6},{6,7},{7,8},{8,9},{9,10},{10,1... | collective-permute-start | bytes 1179656 | tf_op jit(solution)/shard_map/while/body/eval_jaxpr/ppermute | solution.py:22
  146.3 11.1 %collective-permute-start = (bf16[1536,128]{1,0:T(8,128)(2,1)S(1)}, bf16[1536,128]{1,0:T(8,128)(2,1)S(1)}, u32[]{:S(2)}, u32[]{:S(2)}) collective-permute-start(bf16[1536,128]{1,0:T(8,128)(2,1)S(1)} %get-tuple-element.337), channel_id=1, source_target_pairs={{0,1},{1,2},{2,3},{3,4},{4,5},{5,6},{6,7},{7,8},{8,9},{9,10},{10,1... | collective-permute-start | bytes 1179656 | tf_op jit(solution)/shard_map/while/body/eval_jaxpr/ppermute | solution.py:22
  162.0 11.1 %collective-permute-start = (bf16[1536,128]{1,0:T(8,128)(2,1)S(1)}, bf16[1536,128]{1,0:T(8,128)(2,1)S(1)}, u32[]{:S(2)}, u32[]{:S(2)}) collective-permute-start(bf16[1536,128]{1,0:T(8,128)(2,1)S(1)} %get-tuple-element.337), channel_id=1, source_target_pairs={{0,1},{1,2},{2,3},{3,4},{4,5},{5,6},{6,7},{7,8},{8,9},{9,10},{10,1... | collective-permute-start | bytes 1179656 | tf_op jit(solution)/shard_map/while/body/eval_jaxpr/ppermute | solution.py:22
  177.7 11.1 %collective-permute-start = (bf16[1536,128]{1,0:T(8,128)(2,1)S(1)}, bf16[1536,128]{1,0:T(8,128)(2,1)S(1)}, u32[]{:S(2)}, u32[]{:S(2)}) collective-permute-start(bf16[1536,128]{1,0:T(8,128)(2,1)S(1)} %get-tuple-element.337), channel_id=1, source_target_pairs={{0,1},{1,2},{2,3},{3,4},{4,5},{5,6},{6,7},{7,8},{8,9},{9,10},{10,1... | collective-permute-start | bytes 1179656 | tf_op jit(solution)/shard_map/while/body/eval_jaxpr/ppermute | solution.py:22
  193.4 11.1 %collective-permute-start = (bf16[1536,128]{1,0:T(8,128)(2,1)S(1)}, bf16[1536,128]{1,0:T(8,128)(2,1)S(1)}, u32[]{:S(2)}, u32[]{:S(2)}) collective-permute-start(bf16[1536,128]{1,0:T(8,128)(2,1)S(1)} %get-tuple-element.337), channel_id=1, source_target_pairs={{0,1},{1,2},{2,3},{3,4},{4,5},{5,6},{6,7},{7,8},{8,9},{9,10},{10,1... | collective-permute-start | bytes 1179656 | tf_op jit(solution)/shard_map/while/body/eval_jaxpr/ppermute | solution.py:22
  209.2 11.1 %collective-permute-start = (bf16[1536,128]{1,0:T(8,128)(2,1)S(1)}, bf16[1536,128]{1,0:T(8,128)(2,1)S(1)}, u32[]{:S(2)}, u32[]{:S(2)}) collective-permute-start(bf16[1536,128]{1,0:T(8,128)(2,1)S(1)} %get-tuple-element.337), channel_id=1, source_target_pairs={{0,1},{1,2},{2,3},{3,4},{4,5},{5,6},{6,7},{7,8},{8,9},{9,10},{10,1... | collective-permute-start | bytes 1179656 | tf_op jit(solution)/shard_map/while/body/eval_jaxpr/ppermute | solution.py:22
  224.9 11.1 %collective-permute-start = (bf16[1536,128]{1,0:T(8,128)(2,1)S(1)}, bf16[1536,128]{1,0:T(8,128)(2,1)S(1)}, u32[]{:S(2)}, u32[]{:S(2)}) collective-permute-start(bf16[1536,128]{1,0:T(8,128)(2,1)S(1)} %get-tuple-element.337), channel_id=1, source_target_pairs={{0,1},{1,2},{2,3},{3,4},{4,5},{5,6},{6,7},{7,8},{8,9},{9,10},{10,1... | collective-permute-start | bytes 1179656 | tf_op jit(solution)/shard_map/while/body/eval_jaxpr/ppermute | solution.py:22
  240.6 11.1 %collective-permute-start = (bf16[1536,128]{1,0:T(8,128)(2,1)S(1)}, bf16[1536,128]{1,0:T(8,128)(2,1)S(1)}, u32[]{:S(2)}, u32[]{:S(2)}) collective-permute-start(bf16[1536,128]{1,0:T(8,128)(2,1)S(1)} %get-tuple-element.337), channel_id=1, source_target_pairs={{0,1},{1,2},{2,3},{3,4},{4,5},{5,6},{6,7},{7,8},{8,9},{9,10},{10,1... | collective-permute-start | bytes 1179656 | tf_op jit(solution)/shard_map/while/body/eval_jaxpr/ppermute | solution.py:22
  256.3 11.1 %collective-permute-start = (bf16[1536,128]{1,0:T(8,128)(2,1)S(1)}, bf16[1536,128]{1,0:T(8,128)(2,1)S(1)}, u32[]{:S(2)}, u32[]{:S(2)}) collective-permute-start(bf16[1536,128]{1,0:T(8,128)(2,1)S(1)} %get-tuple-element.337), channel_id=1, source_target_pairs={{0,1},{1,2},{2,3},{3,4},{4,5},{5,6},{6,7},{7,8},{8,9},{9,10},{10,1... | collective-permute-start | bytes 1179656 | tf_op jit(solution)/shard_map/while/body/eval_jaxpr/ppermute | solution.py:22
  272.1 11.1 %collective-permute-start = (bf16[1536,128]{1,0:T(8,128)(2,1)S(1)}, bf16[1536,128]{1,0:T(8,128)(2,1)S(1)}, u32[]{:S(2)}, u32[]{:S(2)}) collective-permute-start(bf16[1536,128]{1,0:T(8,128)(2,1)S(1)} %get-tuple-element.337), channel_id=1, source_target_pairs={{0,1},{1,2},{2,3},{3,4},{4,5},{5,6},{6,7},{7,8},{8,9},{9,10},{10,1... | collective-permute-start | bytes 1179656 | tf_op jit(solution)/shard_map/while/body/eval_jaxpr/ppermute | solution.py:22
  287.8 11.1 %collective-permute-start = (bf16[1536,128]{1,0:T(8,128)(2,1)S(1)}, bf16[1536,128]{1,0:T(8,128)(2,1)S(1)}, u32[]{:S(2)}, u32[]{:S(2)}) collective-permute-start(bf16[1536,128]{1,0:T(8,128)(2,1)S(1)} %get-tuple-element.337), channel_id=1, source_target_pairs={{0,1},{1,2},{2,3},{3,4},{4,5},{5,6},{6,7},{7,8},{8,9},{9,10},{10,1... | collective-permute-start | bytes 1179656 | tf_op jit(solution)/shard_map/while/body/eval_jaxpr/ppermute | solution.py:22
  303.5 11.1 %collective-permute-start = (bf16[1536,128]{1,0:T(8,128)(2,1)S(1)}, bf16[1536,128]{1,0:T(8,128)(2,1)S(1)}, u32[]{:S(2)}, u32[]{:S(2)}) collective-permute-start(bf16[1536,128]{1,0:T(8,128)(2,1)S(1)} %get-tuple-element.337), channel_id=1, source_target_pairs={{0,1},{1,2},{2,3},{3,4},{4,5},{5,6},{6,7},{7,8},{8,9},{9,10},{10,1... | collective-permute-start | bytes 1179656 | tf_op jit(solution)/shard_map/while/body/eval_jaxpr/ppermute | solution.py:22
  319.2 11.1 %collective-permute-start = (bf16[1536,128]{1,0:T(8,128)(2,1)S(1)}, bf16[1536,128]{1,0:T(8,128)(2,1)S(1)}, u32[]{:S(2)}, u32[]{:S(2)}) collective-permute-start(bf16[1536,128]{1,0:T(8,128)(2,1)S(1)} %get-tuple-element.337), channel_id=1, source_target_pairs={{0,1},{1,2},{2,3},{3,4},{4,5},{5,6},{6,7},{7,8},{8,9},{9,10},{10,1... | collective-permute-start | bytes 1179656 | tf_op jit(solution)/shard_map/while/body/eval_jaxpr/ppermute | solution.py:22
  334.9 11.1 %collective-permute-start = (bf16[1536,128]{1,0:T(8,128)(2,1)S(1)}, bf16[1536,128]{1,0:T(8,128)(2,1)S(1)}, u32[]{:S(2)}, u32[]{:S(2)}) collective-permute-start(bf16[1536,128]{1,0:T(8,128)(2,1)S(1)} %get-tuple-element.337), channel_id=1, source_target_pairs={{0,1},{1,2},{2,3},{3,4},{4,5},{5,6},{6,7},{7,8},{8,9},{9,10},{10,1... | collective-permute-start | bytes 1179656 | tf_op jit(solution)/shard_map/while/body/eval_jaxpr/ppermute | solution.py:22
  350.7 11.1 %collective-permute-start = (bf16[1536,128]{1,0:T(8,128)(2,1)S(1)}, bf16[1536,128]{1,0:T(8,128)(2,1)S(1)}, u32[]{:S(2)}, u32[]{:S(2)}) collective-permute-start(bf16[1536,128]{1,0:T(8,128)(2,1)S(1)} %get-tuple-element.337), channel_id=1, source_target_pairs={{0,1},{1,2},{2,3},{3,4},{4,5},{5,6},{6,7},{7,8},{8,9},{9,10},{10,1... | collective-permute-start | bytes 1179656 | tf_op jit(solution)/shard_map/while/body/eval_jaxpr/ppermute | solution.py:22
  366.4 11.1 %collective-permute-start = (bf16[1536,128]{1,0:T(8,128)(2,1)S(1)}, bf16[1536,128]{1,0:T(8,128)(2,1)S(1)}, u32[]{:S(2)}, u32[]{:S(2)}) collective-permute-start(bf16[1536,128]{1,0:T(8,128)(2,1)S(1)} %get-tuple-element.337), channel_id=1, source_target_pairs={{0,1},{1,2},{2,3},{3,4},{4,5},{5,6},{6,7},{7,8},{8,9},{9,10},{10,1... | collective-permute-start | bytes 1179656 | tf_op jit(solution)/shard_map/while/body/eval_jaxpr/ppermute | solution.py:22
  382.1 11.1 %collective-permute-start = (bf16[1536,128]{1,0:T(8,128)(2,1)S(1)}, bf16[1536,128]{1,0:T(8,128)(2,1)S(1)}, u32[]{:S(2)}, u32[]{:S(2)}) collective-permute-start(bf16[1536,128]{1,0:T(8,128)(2,1)S(1)} %get-tuple-element.337), channel_id=1, source_target_pairs={{0,1},{1,2},{2,3},{3,4},{4,5},{5,6},{6,7},{7,8},{8,9},{9,10},{10,1... | collective-permute-start | bytes 1179656 | tf_op jit(solution)/shard_map/while/body/eval_jaxpr/ppermute | solution.py:22
  397.8 11.1 %collective-permute-start = (bf16[1536,128]{1,0:T(8,128)(2,1)S(1)}, bf16[1536,128]{1,0:T(8,128)(2,1)S(1)}, u32[]{:S(2)}, u32[]{:S(2)}) collective-permute-start(bf16[1536,128]{1,0:T(8,128)(2,1)S(1)} %get-tuple-element.337), channel_id=1, source_target_pairs={{0,1},{1,2},{2,3},{3,4},{4,5},{5,6},{6,7},{7,8},{8,9},{9,10},{10,1... | collective-permute-start | bytes 1179656 | tf_op jit(solution)/shard_map/while/body/eval_jaxpr/ppermute | solution.py:22
  413.6 11.1 %collective-permute-start = (bf16[1536,128]{1,0:T(8,128)(2,1)S(1)}, bf16[1536,128]{1,0:T(8,128)(2,1)S(1)}, u32[]{:S(2)}, u32[]{:S(2)}) collective-permute-start(bf16[1536,128]{1,0:T(8,128)(2,1)S(1)} %get-tuple-element.337), channel_id=1, source_target_pairs={{0,1},{1,2},{2,3},{3,4},{4,5},{5,6},{6,7},{7,8},{8,9},{9,10},{10,1... | collective-permute-start | bytes 1179656 | tf_op jit(solution)/shard_map/while/body/eval_jaxpr/ppermute | solution.py:22
  429.3 11.1 %collective-permute-start = (bf16[1536,128]{1,0:T(8,128)(2,1)S(1)}, bf16[1536,128]{1,0:T(8,128)(2,1)S(1)}, u32[]{:S(2)}, u32[]{:S(2)}) collective-permute-start(bf16[1536,128]{1,0:T(8,128)(2,1)S(1)} %get-tuple-element.337), channel_id=1, source_target_pairs={{0,1},{1,2},{2,3},{3,4},{4,5},{5,6},{6,7},{7,8},{8,9},{9,10},{10,1... | collective-permute-start | bytes 1179656 | tf_op jit(solution)/shard_map/while/body/eval_jaxpr/ppermute | solution.py:22
  445.0 11.1 %collective-permute-start = (bf16[1536,128]{1,0:T(8,128)(2,1)S(1)}, bf16[1536,128]{1,0:T(8,128)(2,1)S(1)}, u32[]{:S(2)}, u32[]{:S(2)}) collective-permute-start(bf16[1536,128]{1,0:T(8,128)(2,1)S(1)} %get-tuple-element.337), channel_id=1, source_target_pairs={{0,1},{1,2},{2,3},{3,4},{4,5},{5,6},{6,7},{7,8},{8,9},{9,10},{10,1... | collective-permute-start | bytes 1179656 | tf_op jit(solution)/shard_map/while/body/eval_jaxpr/ppermute | solution.py:22
  460.7 11.1 %collective-permute-start = (bf16[1536,128]{1,0:T(8,128)(2,1)S(1)}, bf16[1536,128]{1,0:T(8,128)(2,1)S(1)}, u32[]{:S(2)}, u32[]{:S(2)}) collective-permute-start(bf16[1536,128]{1,0:T(8,128)(2,1)S(1)} %get-tuple-element.337), channel_id=1, source_target_pairs={{0,1},{1,2},{2,3},{3,4},{4,5},{5,6},{6,7},{7,8},{8,9},{9,10},{10,1... | collective-permute-start | bytes 1179656 | tf_op jit(solution)/shard_map/while/body/eval_jaxpr/ppermute | solution.py:22
  476.4 11.1 %collective-permute-start = (bf16[1536,128]{1,0:T(8,128)(2,1)S(1)}, bf16[1536,128]{1,0:T(8,128)(2,1)S(1)}, u32[]{:S(2)}, u32[]{:S(2)}) collective-permute-start(bf16[1536,128]{1,0:T(8,128)(2,1)S(1)} %get-tuple-element.337), channel_id=1, source_target_pairs={{0,1},{1,2},{2,3},{3,4},{4,5},{5,6},{6,7},{7,8},{8,9},{9,10},{10,1... | collective-permute-start | bytes 1179656 | tf_op jit(solution)/shard_map/while/body/eval_jaxpr/ppermute | solution.py:22
  495.9 11.2 %collective-permute-start.2 = (bf16[1536,128]{1,0:T(8,128)(2,1)S(1)}, bf16[1536,128]{1,0:T(8,128)(2,1)S(1)}, u32[]{:S(2)}, u32[]{:S(2)}) collective-permute-start(bf16[1536,128]{1,0:T(8,128)(2,1)S(1)} %get-tuple-element.364), channel_id=1, source_target_pairs={{0,1},{1,2},{2,3},{3,4},{4,5},{5,6},{6,7},{7,8},{8,9},{9,10},{10,1... | collective-permute-start | bytes 1179656 | tf_op jit(solution)/shard_map/while/body/eval_jaxpr/ppermute | solution.py:22
  527.4 11.1 %collective-permute-start.2 = (bf16[1536,128]{1,0:T(8,128)(2,1)S(1)}, bf16[1536,128]{1,0:T(8,128)(2,1)S(1)}, u32[]{:S(2)}, u32[]{:S(2)}) collective-permute-start(bf16[1536,128]{1,0:T(8,128)(2,1)S(1)} %get-tuple-element.364), channel_id=1, source_target_pairs={{0,1},{1,2},{2,3},{3,4},{4,5},{5,6},{6,7},{7,8},{8,9},{9,10},{10,1... | collective-permute-start | bytes 1179656 | tf_op jit(solution)/shard_map/while/body/eval_jaxpr/ppermute | solution.py:22
  543.1 11.1 %collective-permute-start.2 = (bf16[1536,128]{1,0:T(8,128)(2,1)S(1)}, bf16[1536,128]{1,0:T(8,128)(2,1)S(1)}, u32[]{:S(2)}, u32[]{:S(2)}) collective-permute-start(bf16[1536,128]{1,0:T(8,128)(2,1)S(1)} %get-tuple-element.364), channel_id=1, source_target_pairs={{0,1},{1,2},{2,3},{3,4},{4,5},{5,6},{6,7},{7,8},{8,9},{9,10},{10,1... | collective-permute-start | bytes 1179656 | tf_op jit(solution)/shard_map/while/body/eval_jaxpr/ppermute | solution.py:22
  558.9 11.1 %collective-permute-start.2 = (bf16[1536,128]{1,0:T(8,128)(2,1)S(1)}, bf16[1536,128]{1,0:T(8,128)(2,1)S(1)}, u32[]{:S(2)}, u32[]{:S(2)}) collective-permute-start(bf16[1536,128]{1,0:T(8,128)(2,1)S(1)} %get-tuple-element.364), channel_id=1, source_target_pairs={{0,1},{1,2},{2,3},{3,4},{4,5},{5,6},{6,7},{7,8},{8,9},{9,10},{10,1... | collective-permute-start | bytes 1179656 | tf_op jit(solution)/shard_map/while/body/eval_jaxpr/ppermute | solution.py:22
  574.6 11.1 %collective-permute-start.2 = (bf16[1536,128]{1,0:T(8,128)(2,1)S(1)}, bf16[1536,128]{1,0:T(8,128)(2,1)S(1)}, u32[]{:S(2)}, u32[]{:S(2)}) collective-permute-start(bf16[1536,128]{1,0:T(8,128)(2,1)S(1)} %get-tuple-element.364), channel_id=1, source_target_pairs={{0,1},{1,2},{2,3},{3,4},{4,5},{5,6},{6,7},{7,8},{8,9},{9,10},{10,1... | collective-permute-start | bytes 1179656 | tf_op jit(solution)/shard_map/while/body/eval_jaxpr/ppermute | solution.py:22
  590.3 11.1 %collective-permute-start.2 = (bf16[1536,128]{1,0:T(8,128)(2,1)S(1)}, bf16[1536,128]{1,0:T(8,128)(2,1)S(1)}, u32[]{:S(2)}, u32[]{:S(2)}) collective-permute-start(bf16[1536,128]{1,0:T(8,128)(2,1)S(1)} %get-tuple-element.364), channel_id=1, source_target_pairs={{0,1},{1,2},{2,3},{3,4},{4,5},{5,6},{6,7},{7,8},{8,9},{9,10},{10,1... | collective-permute-start | bytes 1179656 | tf_op jit(solution)/shard_map/while/body/eval_jaxpr/ppermute | solution.py:22
  606.0 11.1 %collective-permute-start.2 = (bf16[1536,128]{1,0:T(8,128)(2,1)S(1)}, bf16[1536,128]{1,0:T(8,128)(2,1)S(1)}, u32[]{:S(2)}, u32[]{:S(2)}) collective-permute-start(bf16[1536,128]{1,0:T(8,128)(2,1)S(1)} %get-tuple-element.364), channel_id=1, source_target_pairs={{0,1},{1,2},{2,3},{3,4},{4,5},{5,6},{6,7},{7,8},{8,9},{9,10},{10,1... | collective-permute-start | bytes 1179656 | tf_op jit(solution)/shard_map/while/body/eval_jaxpr/ppermute | solution.py:22
  621.8 11.1 %collective-permute-start.2 = (bf16[1536,128]{1,0:T(8,128)(2,1)S(1)}, bf16[1536,128]{1,0:T(8,128)(2,1)S(1)}, u32[]{:S(2)}, u32[]{:S(2)}) collective-permute-start(bf16[1536,128]{1,0:T(8,128)(2,1)S(1)} %get-tuple-element.364), channel_id=1, source_target_pairs={{0,1},{1,2},{2,3},{3,4},{4,5},{5,6},{6,7},{7,8},{8,9},{9,10},{10,1... | collective-permute-start | bytes 1179656 | tf_op jit(solution)/shard_map/while/body/eval_jaxpr/ppermute | solution.py:22
  637.5 11.1 %collective-permute-start.2 = (bf16[1536,128]{1,0:T(8,128)(2,1)S(1)}, bf16[1536,128]{1,0:T(8,128)(2,1)S(1)}, u32[]{:S(2)}, u32[]{:S(2)}) collective-permute-start(bf16[1536,128]{1,0:T(8,128)(2,1)S(1)} %get-tuple-element.364), channel_id=1, source_target_pairs={{0,1},{1,2},{2,3},{3,4},{4,5},{5,6},{6,7},{7,8},{8,9},{9,10},{10,1... | collective-permute-start | bytes 1179656 | tf_op jit(solution)/shard_map/while/body/eval_jaxpr/ppermute | solution.py:22
  653.2 11.1 %collective-permute-start.2 = (bf16[1536,128]{1,0:T(8,128)(2,1)S(1)}, bf16[1536,128]{1,0:T(8,128)(2,1)S(1)}, u32[]{:S(2)}, u32[]{:S(2)}) collective-permute-start(bf16[1536,128]{1,0:T(8,128)(2,1)S(1)} %get-tuple-element.364), channel_id=1, source_target_pairs={{0,1},{1,2},{2,3},{3,4},{4,5},{5,6},{6,7},{7,8},{8,9},{9,10},{10,1... | collective-permute-start | bytes 1179656 | tf_op jit(solution)/shard_map/while/body/eval_jaxpr/ppermute | solution.py:22
  668.9 11.1 %collective-permute-start.2 = (bf16[1536,128]{1,0:T(8,128)(2,1)S(1)}, bf16[1536,128]{1,0:T(8,128)(2,1)S(1)}, u32[]{:S(2)}, u32[]{:S(2)}) collective-permute-start(bf16[1536,128]{1,0:T(8,128)(2,1)S(1)} %get-tuple-element.364), channel_id=1, source_target_pairs={{0,1},{1,2},{2,3},{3,4},{4,5},{5,6},{6,7},{7,8},{8,9},{9,10},{10,1... | collective-permute-start | bytes 1179656 | tf_op jit(solution)/shard_map/while/body/eval_jaxpr/ppermute | solution.py:22
  684.6 11.1 %collective-permute-start.2 = (bf16[1536,128]{1,0:T(8,128)(2,1)S(1)}, bf16[1536,128]{1,0:T(8,128)(2,1)S(1)}, u32[]{:S(2)}, u32[]{:S(2)}) collective-permute-start(bf16[1536,128]{1,0:T(8,128)(2,1)S(1)} %get-tuple-element.364), channel_id=1, source_target_pairs={{0,1},{1,2},{2,3},{3,4},{4,5},{5,6},{6,7},{7,8},{8,9},{9,10},{10,1... | collective-permute-start | bytes 1179656 | tf_op jit(solution)/shard_map/while/body/eval_jaxpr/ppermute | solution.py:22
  700.4 11.1 %collective-permute-start.2 = (bf16[1536,128]{1,0:T(8,128)(2,1)S(1)}, bf16[1536,128]{1,0:T(8,128)(2,1)S(1)}, u32[]{:S(2)}, u32[]{:S(2)}) collective-permute-start(bf16[1536,128]{1,0:T(8,128)(2,1)S(1)} %get-tuple-element.364), channel_id=1, source_target_pairs={{0,1},{1,2},{2,3},{3,4},{4,5},{5,6},{6,7},{7,8},{8,9},{9,10},{10,1... | collective-permute-start | bytes 1179656 | tf_op jit(solution)/shard_map/while/body/eval_jaxpr/ppermute | solution.py:22
  716.1 11.1 %collective-permute-start.2 = (bf16[1536,128]{1,0:T(8,128)(2,1)S(1)}, bf16[1536,128]{1,0:T(8,128)(2,1)S(1)}, u32[]{:S(2)}, u32[]{:S(2)}) collective-permute-start(bf16[1536,128]{1,0:T(8,128)(2,1)S(1)} %get-tuple-element.364), channel_id=1, source_target_pairs={{0,1},{1,2},{2,3},{3,4},{4,5},{5,6},{6,7},{7,8},{8,9},{9,10},{10,1... | collective-permute-start | bytes 1179656 | tf_op jit(solution)/shard_map/while/body/eval_jaxpr/ppermute | solution.py:22
  731.8 11.1 %collective-permute-start.2 = (bf16[1536,128]{1,0:T(8,128)(2,1)S(1)}, bf16[1536,128]{1,0:T(8,128)(2,1)S(1)}, u32[]{:S(2)}, u32[]{:S(2)}) collective-permute-start(bf16[1536,128]{1,0:T(8,128)(2,1)S(1)} %get-tuple-element.364), channel_id=1, source_target_pairs={{0,1},{1,2},{2,3},{3,4},{4,5},{5,6},{6,7},{7,8},{8,9},{9,10},{10,1... | collective-permute-start | bytes 1179656 | tf_op jit(solution)/shard_map/while/body/eval_jaxpr/ppermute | solution.py:22
  747.5 11.1 %collective-permute-start.2 = (bf16[1536,128]{1,0:T(8,128)(2,1)S(1)}, bf16[1536,128]{1,0:T(8,128)(2,1)S(1)}, u32[]{:S(2)}, u32[]{:S(2)}) collective-permute-start(bf16[1536,128]{1,0:T(8,128)(2,1)S(1)} %get-tuple-element.364), channel_id=1, source_target_pairs={{0,1},{1,2},{2,3},{3,4},{4,5},{5,6},{6,7},{7,8},{8,9},{9,10},{10,1... | collective-permute-start | bytes 1179656 | tf_op jit(solution)/shard_map/while/body/eval_jaxpr/ppermute | solution.py:22
  763.3 11.1 %collective-permute-start.2 = (bf16[1536,128]{1,0:T(8,128)(2,1)S(1)}, bf16[1536,128]{1,0:T(8,128)(2,1)S(1)}, u32[]{:S(2)}, u32[]{:S(2)}) collective-permute-start(bf16[1536,128]{1,0:T(8,128)(2,1)S(1)} %get-tuple-element.364), channel_id=1, source_target_pairs={{0,1},{1,2},{2,3},{3,4},{4,5},{5,6},{6,7},{7,8},{8,9},{9,10},{10,1... | collective-permute-start | bytes 1179656 | tf_op jit(solution)/shard_map/while/body/eval_jaxpr/ppermute | solution.py:22
  779.0 11.1 %collective-permute-start.2 = (bf16[1536,128]{1,0:T(8,128)(2,1)S(1)}, bf16[1536,128]{1,0:T(8,128)(2,1)S(1)}, u32[]{:S(2)}, u32[]{:S(2)}) collective-permute-start(bf16[1536,128]{1,0:T(8,128)(2,1)S(1)} %get-tuple-element.364), channel_id=1, source_target_pairs={{0,1},{1,2},{2,3},{3,4},{4,5},{5,6},{6,7},{7,8},{8,9},{9,10},{10,1... | collective-permute-start | bytes 1179656 | tf_op jit(solution)/shard_map/while/body/eval_jaxpr/ppermute | solution.py:22
  794.7 11.1 %collective-permute-start.2 = (bf16[1536,128]{1,0:T(8,128)(2,1)S(1)}, bf16[1536,128]{1,0:T(8,128)(2,1)S(1)}, u32[]{:S(2)}, u32[]{:S(2)}) collective-permute-start(bf16[1536,128]{1,0:T(8,128)(2,1)S(1)} %get-tuple-element.364), channel_id=1, source_target_pairs={{0,1},{1,2},{2,3},{3,4},{4,5},{5,6},{6,7},{7,8},{8,9},{9,10},{10,1... | collective-permute-start | bytes 1179656 | tf_op jit(solution)/shard_map/while/body/eval_jaxpr/ppermute | solution.py:22
  810.4 11.1 %collective-permute-start.2 = (bf16[1536,128]{1,0:T(8,128)(2,1)S(1)}, bf16[1536,128]{1,0:T(8,128)(2,1)S(1)}, u32[]{:S(2)}, u32[]{:S(2)}) collective-permute-start(bf16[1536,128]{1,0:T(8,128)(2,1)S(1)} %get-tuple-element.364), channel_id=1, source_target_pairs={{0,1},{1,2},{2,3},{3,4},{4,5},{5,6},{6,7},{7,8},{8,9},{9,10},{10,1... | collective-permute-start | bytes 1179656 | tf_op jit(solution)/shard_map/while/body/eval_jaxpr/ppermute | solution.py:22
  (79 other events, 822.1 us)
where the time goes:
time: 993 us; the launch traced here: 984 us
  waiting for transfers between devices  663 us (67%)
  matrix products  278 us (28%)
  other arithmetic  18.4 us (2%)
  starting transfers between devices  15.9 us (2%)
    ppermute x62, waiting for transfers between devices, visit_step(): v_vis = lax.ppermute(v_vis, 'row', shift_pairs)  663 us
    dot_general x64, matrix products, kernel_product(): return jnp.dot(kern_tile, v_cols, preferred_element_type=jnp.float32)  273 us
  transfers between devices with their start and end apart: 124, of which 62 were waited for; matrix products, arithmetic and copies ran while one was open for 0% of the time, Pallas kernels for 0%

commit v1 on v0

v1 whole, which is shorter than its diff:
```python
import functools

import jax
import jax.numpy as jnp
from jax import lax
from jax.experimental import pallas as pl
from jax.experimental.pallas import tpu as pltpu
from jax.sharding import PartitionSpec as P

BF16 = jnp.bfloat16
F32 = jnp.float32
LOG2E = 1.4426950408889634
COL_TILE = 512
ROW_TILE = 768


def split3(val):
    high = val.astype(BF16).astype(F32)
    mid = (val - high).astype(BF16).astype(F32)
    low = (val - high) - mid
    return high, mid, low


def pass_kernel(scal_ref, own_ref, vis_ref, vt_ref, out_ref):
    rows, feat2 = vis_ref.shape
    own = own_ref.shape[1]
    coef = scal_ref[0]
    scale = scal_ref[1]
    cap = jnp.full((ROW_TILE, COL_TILE), scale, F32).astype(BF16)

    @pl.when(pl.program_id(0) == 0)
    def _():
        out_ref[...] = jnp.zeros_like(out_ref)

    for col in range(0, own, COL_TILE):
        total = out_ref[:, pl.ds(col, COL_TILE)]
        for row in range(0, rows, ROW_TILE):
            neg_dist = jnp.dot(vis_ref[pl.ds(row, ROW_TILE), :], own_ref[:, pl.ds(col, COL_TILE)], preferred_element_type=F32)
            tile = jnp.minimum((jnp.exp2(neg_dist * coef) * scale).astype(BF16), cap)
            total = total + jnp.dot(vt_ref[:, pl.ds(row, ROW_TILE)], tile, preferred_element_type=F32)
        out_ref[:, pl.ds(col, COL_TILE)] = total


def kernel_pass(scal, own_side, vis_side, vt_all):
    n_all, feat2 = vis_side.shape
    own = own_side.shape[1]
    n_col = vt_all.shape[0]
    return pl.pallas_call(
        pass_kernel,
        grid=(n_all // own,),
        in_specs=[
            pl.BlockSpec(memory_space=pltpu.SMEM),
            pl.BlockSpec((feat2, own), lambda i: (0, 0)),
            pl.BlockSpec((own, feat2), lambda i: (i, 0)),
            pl.BlockSpec((n_col, own), lambda i: (0, i)),
        ],
        out_specs=pl.BlockSpec((n_col, own), lambda i: (0, 0)),
        out_shape=jax.ShapeDtypeStruct((n_col, own), F32),
        cost_estimate=pl.CostEstimate(flops=2 * n_all * own * feat2, bytes_accessed=2 * n_all * feat2, transcendentals=n_all * own),
        name="kernel_pass",
    )(scal, own_side, vis_side, vt_all)


def solution(mesh):
    def local_program(x_loc, v_loc, length_scale, out_scale):
        ell, scale = length_scale[0], out_scale[0]
        shrink = jnp.where(ell > 2.0**64, 2.0**-70, jnp.where(ell > 2.0**32, 2.0**-32, 1.0)).astype(F32)
        ell = ell * shrink
        coef = LOG2E / (2.0 * ell * ell)
        scal = jnp.stack([coef, scale])
        x_f = x_loc.astype(F32) * shrink
        parts = split3(jnp.sum(jnp.square(x_f), axis=1))
        rows = x_loc.shape[0]
        one = jnp.ones((rows,), F32)
        pad = jnp.zeros((rows, x_loc.shape[1] - 6), F32)
        vis = jnp.concatenate([x_f, jnp.stack([*parts, one, one, one], axis=1), pad], axis=1).astype(BF16)
        own = jnp.concatenate([2.0 * x_f, jnp.stack([-one, -one, -one, *(-p for p in parts)], axis=1), pad], axis=1).astype(BF16).T
        vis_all = lax.all_gather(vis, "row", axis=0, tiled=True)
        vt_all = lax.all_gather(v_loc, "row", axis=0, tiled=True).T
        first = kernel_pass(scal, own, vis_all, vt_all).astype(BF16)
        yt_all = lax.all_gather(first, "row", axis=1, tiled=True)
        return kernel_pass(scal, own, vis_all, yt_all).T

    row_spec = P(("task", "row"), None)
    return jax.shard_map(local_program, mesh=mesh, in_specs=(row_spec, row_spec, P("task"), P("task")), out_specs=row_spec, check_vma=False)
```

time: 993 us -> 343 us (0.35)
  waiting for transfers between devices: 663 us -> 158 us
  matrix products: 278 us -> 0 us
  Pallas kernels: 0 us -> 158 us
  starting transfers between devices: 15.9 us -> 0.13 us
  other arithmetic: 18.4 us -> 4.51 us
  between operations: 1.35 us -> 14.5 us
    ppermute x124 -> x0, waiting for transfers between devices: 663 us -> none  [the longest x62 663 us: visit_step(): v_vis = lax.ppermute(v_vis, 'row', shift_pairs)]
    dot_general x65 -> x0, matrix products: 278 us -> none  [the longest x64 273 us: kernel_product(): return jnp.dot(kern_tile, v_cols, preferred_element_type=jnp.float32)]
    pallas_call x0 -> x2, Pallas kernels: none -> 158 us  [kernel_pass(): pl.pallas_call(pass_kernel, grid=(n_all // own,), in_specs=[pl.BlockSpec(...]
    all_gather x0 -> x3, waiting for transfers between devices: none -> 157 us  [the longest x1 88.1 us: local_program(): vis_all = lax.all_gather(vis, 'row', axis=0, tiled=True)]
    reduce_sum x63 -> x0, other arithmetic: 18.4 us -> none  [the longest x62 17.1 us: visit_step(): norm_vis = jnp.sum(jnp.square(x_vis.astype(jnp.float32)), axis=1)]
    ppermute x124 -> x0, starting transfers between devices: 15.9 us -> none  [the longest x62 9.34 us: visit_step(): x_vis = lax.ppermute(x_vis, 'row', shift_pairs)]
  transfers between devices with their start and end apart: 124 -> 3, of which waited for: 62 -> 3; matrix products, arithmetic and copies ran while one was open for 0% -> 3% of each run, Pallas kernels for 0% -> 0%
where the time goes in v1:
time: 343 us; the launch traced here: 342 us
  waiting for transfers between devices  158 us (46%)
  Pallas kernels  158 us (46%)
  between operations  14.5 us (4%)
  local copies, waits for them, and re-layouts  7.5 us (2%)
  other arithmetic  4.51 us (1%)
    pallas_call x2, Pallas kernels, kernel_pass(): pl.pallas_call(pass_kernel, grid=(n_all // own,), in_specs=[pl.BlockSpec(...  158 us
    all_gather x1, waiting for transfers between devices, local_program(): vis_all = lax.all_gather(vis, 'row', axis=0, tiled=True)  88.1 us
    all_gather x1, waiting for transfers between devices, local_program(): yt_all = lax.all_gather(first, 'row', axis=1, tiled=True)  37.1 us
    all_gather x1, waiting for transfers between devices, local_program(): vt_all = lax.all_gather(v_loc, 'row', axis=0, tiled=True).T  32 us
  transfers between devices with their start and end apart: 3, of which 3 were waited for; matrix products, arithmetic and copies ran while one was open for 3% of the time, Pallas kernels for 0%

profile of v1, /device:TPU:97, one launch (start us, length us, event | category | flops | bytes accessed | tf_op | source)
XLA Modules:
  0.0 342.4 jit_solution(4449294330731578859)
XLA Ops:
  6.5 0.0 all-gather.6.cloned.1.call-start
  6.6 0.7 all-gather.6.cloned.1.call-update
  7.3 0.1 all-gather.4.cloned.1.call-start
  8.0 2.1 fusion.2
  10.1 0.3 copy.11
  10.4 0.3 copy.12
  10.7 0.3 fusion.4
  11.0 0.1 broadcast_in_dim.3
  11.0 0.1 concatenate.16
  11.1 0.1 stack_broadcast_in_dim.3
  11.1 3.6 %concatenate.17 = bf16[1536,256]{1,0:T(8,128)(2,1)} concatenate(bf16[1536,128]{1,0:T(8,128)(2,1)} %get-tuple-element.10, bf16[1536,1]{1,0:T(8,128)(2,1)S(1)} %copy.11, bf16[1536,1]{1,0:T(8,128)(2,1)S(1)} %get-tuple-element.8, bf16[1536,1]{1,0:T(8,128)(2,1)S(1)} %get-tuple-element.5, bf16[1536,1]{1,0:T(8,128)(2,1)S(1)} %stack_broadcast_in_dim.3, bf16[1536,2]{1,0:T(8,128)(2,1)S(1)} %concatenate.16, ...), dimensions={1} | concatenate | bytes 1572864 | tf_op jit(solution)/shard_map/concatenate | solution.py:76
  14.8 0.0 copy-start
  14.8 0.1 all-gather.4.cloned.1.call-update
  14.8 0.1 all-gather.8.cloned.1.call-start
  14.9 0.1 concatenate.14
  14.9 0.1 stack.8
  15.0 0.7 copy-done
  15.7 1.2 concatenate.15
  16.9 1.2 copy.15.own_ref
  18.8 0.6 pad_maximum_fusion.scal_ref
  19.4 32.0 %all-gather.6.cloned.1.call-done = bf16[49152,16]{0,1:T(8,128)(2,1)} async-done(((bf16[1536,16]{0,1:T(8,128)(2,1)}), bf16[49152,16]{0,1:T(8,128)(2,1)}) %all-gather.6.cloned.1.call-update) | async-done | bytes 1572880 | tf_op jit(solution)/shard_map/all_gather | solution.py:79
  51.4 88.1 %all-gather.4.cloned.1.call-done.vis_ref = bf16[49152,256]{1,0:T(8,128)(2,1)} async-done(((bf16[1536,256]{1,0:T(8,128)(2,1)}), bf16[49152,256]{1,0:T(8,128)(2,1)}) %all-gather.4.cloned.1.call-update) | async-done | bytes 25165840 | tf_op jit(solution)/shard_map/all_gather | solution.py:78
  139.5 78.8 %kernel_pass.2 = f32[16,1536]{1,0:T(8,128)} custom-call(f32[2]{0:T(128)} %pad_maximum_fusion.scal_ref, bf16[256,1536]{1,0:T(8,128)(2,1)} %copy.15.own_ref, bf16[49152,256]{1,0:T(8,128)(2,1)} %all-gather.4.cloned.1.call-done.vis_ref, bf16[16,49152]{1,0:T(8,128)(2,1)} %bitcast.9), custom_call_target="tpu_custom_call" | custom-call | flops 38654705664 | bytes 25165824 | tf_op jit(solution)/shard_map/kernel_pass/pallas_call | solution.py:48
  218.4 1.5 convert_element_type.117
  219.9 0.1 all-gather.8.cloned.1.call-update
  219.9 37.1 %all-gather.8.cloned.1.call-done.vt_ref = bf16[16,49152]{1,0:T(8,128)(2,1)} async-done(((bf16[16,1536]{1,0:T(8,128)(2,1)}), bf16[16,49152]{1,0:T(8,128)(2,1)}) %all-gather.8.cloned.1.call-update) | async-done | bytes 1572880 | tf_op jit(solution)/shard_map/all_gather | solution.py:81
  257.0 78.8 %kernel_pass.3 = f32[16,1536]{1,0:T(8,128)} custom-call(f32[2]{0:T(128)} %pad_maximum_fusion.scal_ref, bf16[256,1536]{1,0:T(8,128)(2,1)} %copy.15.own_ref, bf16[49152,256]{1,0:T(8,128)(2,1)} %all-gather.4.cloned.1.call-done.vis_ref, bf16[16,49152]{1,0:T(8,128)(2,1)} %all-gather.8.cloned.1.call-done.vt_ref), custom_call_target="tpu_custom_call" | custom-call | flops 38654705664 | bytes 25165824 | tf_op jit(solution)/shard_map/kernel_pass/pallas_call | solution.py:48
  (2 shorter events, 0.0 us)
Async XLA Ops:
  6.5 44.9 %all-gather.6.cloned.1.call-start = ((), (), s32[]{:S(2)}) async-start(), calls=%async_computation.1 | async-start | bytes 1622016 | tf_op jit(solution)/shard_map/all_gather | solution.py:79
  7.3 132.2 %all-gather.4.cloned.1.call-start = ((), (), s32[]{:S(2)}) async-start(), calls=%async_computation | async-start | bytes 25952256 | tf_op jit(solution)/shard_map/all_gather | solution.py:78
  14.8 1.0 copy-start
  14.8 242.2 %all-gather.8.cloned.1.call-start = ((), (), s32[]{:S(2)}) async-start(), calls=%async_computation.2 | async-start | bytes 1622016 | tf_op jit(solution)/shard_map/all_gather | solution.py:81
Sparse Core Ops, SparseCore 0:
  9.4 41.9 all-gather.5
  53.5 86.0 all-gather.3
  220.1 36.8 all-gather.7

commit v2 on v0

v2 whole, which is shorter than its diff:
```python
import math

import jax
import jax.numpy as jnp
from jax import lax
from jax.experimental import pallas as pl
from jax.experimental.pallas import tpu as pltpu
from jax.sharding import PartitionSpec as P

BF16 = jnp.bfloat16
F32 = jnp.float32
LOG2E = 1.4426950408889634
TILE = 512
LANES = 128
LAG = 1
STEP = ((1, 0), (0, 1), (-1, 0), (0, -1))
WAVES = (
    (0, 0, 1, 0),
    (2, 0, -1, 0),
    (3, 0, 0, 1),
    (1, 0, 0, -1),
    (0, 1, 2, 0),
    (3, 1, 1, 1),
    (1, 1, 1, -1),
    (3, 2, -1, 1),
    (1, 2, -1, -1),
    (3, 3, 0, 2),
    (3, 5, 2, 1),
    (1, 5, 2, -1),
    (3, 6, 1, 2),
    (3, 8, -1, 2),
    (3, 11, 2, 2),
)
AHEAD = 4


def split3(val):
    high = val.astype(BF16).astype(F32)
    mid = (val - high).astype(BF16).astype(F32)
    low = (val - high) - mid
    return high, mid, low


def make_kernel(n_row, own):
    side = math.isqrt(n_row // 2)
    n_slot = side * side
    quarter = own // 4
    n_c, n_r = own // TILE, own // TILE
    units = [(c, r) for c in range(n_c) for r in range(n_r)]
    n_u = len(units)

    def kernel(
        scal_ref, x_ref, vt_ref, out_ref, xbuf, abuf, vbuf, ybuf, wbuf, total,
        load_sem, send_sem, recv_sem, sib_send, sib_recv, ysend_sem, yrecv_sem, ysib_send, ysib_recv,
    ):
        me = lax.axis_index("row")
        core, chip = me % 2, me // 2
        cx, cy = chip % side, chip // side

        def chip_id(dx, dy):
            return {"row": (((cy + dy + side) % side) * side + (cx + dx + side) % side) * 2 + core}

        sibling = {"row": chip * 2 + 1 - core}

        load_x = pltpu.make_async_copy(x_ref, xbuf.at[0, 0], load_sem.at[0])
        load_v = pltpu.make_async_copy(vt_ref, vbuf.at[0, 1, pl.ds(0, 16)], load_sem.at[1])
        load_x.start()
        load_v.start()

        barrier = pltpu.get_barrier_semaphore()
        for k in range(1, n_slot):
            pl.semaphore_signal(barrier, inc=1, device_id=chip_id(k % side, k // side))
        pl.semaphore_signal(barrier, inc=1, device_id=sibling)

        coef, scale, shrink2 = scal_ref[0], scal_ref[1], scal_ref[2]
        cap = jnp.full((TILE, TILE), scale, F32).astype(BF16)
        wbuf[pl.ds(LANES + 16, LANES - 16), :] = jnp.zeros((LANES - 16, own), BF16)

        load_x.wait()
        load_v.wait()
        row_idx = lax.broadcasted_iota(jnp.int32, (16, LANES), 0)
        for r in range(own // LANES):
            x_t = xbuf[0, 0, pl.ds(r * LANES, LANES), :].astype(F32).T
            norm = jnp.sum(x_t * x_t, axis=0, keepdims=True) * shrink2
            parts = [jnp.broadcast_to(p, (16, LANES)) for p in split3(norm)]
            vis = jnp.where(row_idx < 6, 1.0, 0.0)
            mine = jnp.where(row_idx < 3, -1.0, 0.0)
            for i, part in enumerate(parts):
                vis = jnp.where(row_idx == i, part, vis)
                mine = jnp.where(row_idx == i + 3, -part, mine)
            vbuf[0, 1, pl.ds(16, 16), pl.ds(r * LANES, LANES)] = vis.astype(BF16)
            wbuf[pl.ds(0, LANES), pl.ds(r * LANES, LANES)] = (x_t * (2.0 * shrink2)).astype(BF16)
            wbuf[pl.ds(LANES, 16), pl.ds(r * LANES, LANES)] = mine.astype(BF16)

        def wave_copies(wave):
            rel, src, _, _ = WAVES[wave]
            copies = []
            for d in range(4):
                q = (d + rel) % 4
                target = chip_id(*STEP[d])
                rows = pl.ds(q * quarter, quarter)
                copies.append(pltpu.make_async_remote_copy(
                    xbuf.at[0, src, rows], xbuf.at[0, wave + 1, rows], send_sem.at[wave % AHEAD, q, 0], recv_sem.at[wave, q, 0], device_id=target))
                copies.append(pltpu.make_async_remote_copy(
                    vbuf.at[0, src + 1, :, rows], vbuf.at[0, wave + 2, :, rows], send_sem.at[wave % AHEAD, q, 1], recv_sem.at[wave, q, 1], device_id=target))
            return copies

        def piece_copies(slot):
            copies = []
            for q in range(4):
                rows = pl.ds(q * quarter, quarter)
                sem = (slot - 1) % AHEAD
                copies.append(pltpu.make_async_remote_copy(
                    xbuf.at[0, slot, rows], xbuf.at[0, slot, rows], send_sem.at[sem, q, 0], recv_sem.at[slot - 1, q, 0], device_id=sibling))
                copies.append(pltpu.make_async_remote_copy(
                    vbuf.at[0, slot + 1, :, rows], vbuf.at[0, slot + 1, :, rows], send_sem.at[sem, q, 1], recv_sem.at[slot - 1, q, 1], device_id=sibling))
            return copies

        def sibling_copies(slot):
            return (
                pltpu.make_async_remote_copy(xbuf.at[0, slot], xbuf.at[1, slot], sib_send.at[0], sib_recv.at[slot, 0], device_id=sibling),
                pltpu.make_async_remote_copy(vbuf.at[0, slot + 1], vbuf.at[1, slot + 1], sib_send.at[1], sib_recv.at[slot, 1], device_id=sibling),
            )

        def y_piece_copy(slot, q, target):
            rows = pl.ds(q * quarter, quarter)
            return pltpu.make_async_remote_copy(
                ybuf.at[0, 1, :, rows], ybuf.at[0, slot + 1, :, rows], ysend_sem.at[slot - 1, q], yrecv_sem.at[slot - 1, q], device_id=target)

        def y_sibling_copy(slot):
            return pltpu.make_async_remote_copy(ybuf.at[0, slot + 1], ybuf.at[1, slot + 1], ysib_send.at[0], ysib_recv.at[slot], device_id=sibling)

        def widen(which, slot, r):
            for lane in range(r * TILE, (r + 1) * TILE, LANES):
                rows = vbuf[which, slot + 1, pl.ds(16, 16), pl.ds(lane, LANES)].astype(F32)
                full = jnp.concatenate([rows, jnp.zeros((LANES - 16, LANES), F32)], axis=0)
                abuf[which, slot, pl.ds(lane, LANES), :] = full.T.astype(BF16)

        def block(buf, which, slot, first):
            gram = {}
            if first:
                widen(which, slot, 0)
            for u in range(n_u + LAG):
                if first and u + 1 < n_r:
                    widen(which, slot, u + 1)
                if u < n_u:
                    c, r = units[u]
                    rows = pl.ds(r * TILE, TILE)
                    lhs = jnp.concatenate([xbuf[which, slot, rows, :], abuf[which, slot, rows, :]], axis=1)
                    gram[u] = jnp.dot(lhs, wbuf[:, pl.ds(c * TILE, TILE)], preferred_element_type=F32)
                if u >= LAG:
                    c, r = units[u - LAG]
                    tile = jnp.minimum((jnp.exp2(gram.pop(u - LAG) * coef) * scale).astype(BF16), cap)
                    lhs = buf[which, slot + 1, pl.ds(0, 16), pl.ds(r * TILE, TILE)]
                    total[:, pl.ds(c * TILE, TILE)] += jnp.dot(lhs, tile, preferred_element_type=F32)

        total[...] = jnp.zeros_like(total)
        pl.semaphore_wait(barrier, n_slot)
        for copy in sibling_copies(0):
            copy.start()
        for wave in range(AHEAD):
            for copy in wave_copies(wave):
                copy.start()

        def first_step(slot, carry):
            @pl.when(slot > 0)
            def _():
                for copy in piece_copies(slot):
                    copy.wait()
                for copy in sibling_copies(slot):
                    copy.wait_send()
                    copy.start()

            for wave in range(AHEAD, n_slot - 1):
                @pl.when(slot == wave - AHEAD + 1)
                def _():
                    for copy in wave_copies(wave):
                        copy.start()

            block(vbuf, 0, slot, True)
            for copy in sibling_copies(slot):
                copy.wait_recv()
            block(vbuf, 1, slot, True)
            return carry

        lax.fori_loop(0, n_slot, first_step, 0)
        ybuf[0, 1] = total[...].astype(BF16)
        total[...] = jnp.zeros_like(total)
        for copy in sibling_copies(n_slot - 1):
            copy.wait_send()

        y_sibling_copy(0).start()
        for wave, (_, _, prim, sec) in enumerate(WAVES):
            for q in range(4):
                (px, py), (sx, sy) = STEP[q], STEP[(q + 1) % 4]
                y_piece_copy(wave + 1, q, chip_id((prim * px + sec * sx) % side, (prim * py + sec * sy) % side)).start()

        def second_step(slot, carry):
            @pl.when(slot > 0)
            def _():
                for q in range(4):
                    y_piece_copy(slot, q, sibling).wait()
                y_sibling_copy(slot).wait_send()
                y_sibling_copy(slot).start()

            block(ybuf, 0, slot, False)
            y_sibling_copy(slot).wait_recv()
            block(ybuf, 1, slot, False)
            return carry

        lax.fori_loop(0, n_slot, second_step, 0)
        out_ref[...] = total[...]
        y_sibling_copy(n_slot - 1).wait_send()

    return kernel, n_slot


def both_passes(n_row, scal, x_loc, vt_loc):
    own, feat = x_loc.shape
    n_col = vt_loc.shape[0]
    kernel, n_slot = make_kernel(n_row, own)
    dma = pltpu.SemaphoreType.DMA
    return pl.pallas_call(
        kernel,
        in_specs=[pl.BlockSpec(memory_space=pltpu.SMEM), pl.BlockSpec(memory_space=pl.ANY), pl.BlockSpec(memory_space=pl.ANY)],
        out_specs=pl.BlockSpec(memory_space=pltpu.VMEM),
        out_shape=jax.ShapeDtypeStruct((n_col, own), F32),
        scratch_shapes=[
            pltpu.VMEM((2, n_slot, own, feat), BF16),
            pltpu.VMEM((2, n_slot, own, feat), BF16),
            pltpu.VMEM((2, n_slot + 1, 32, own), BF16),
            pltpu.VMEM((2, n_slot + 1, n_col, own), BF16),
            pltpu.VMEM((2 * feat, own), BF16),
            pltpu.VMEM((n_col, own), F32),
            dma((2,)),
            dma((AHEAD, 4, 2)),
            dma((n_slot - 1, 4, 2)),
            dma((2,)),
            dma((n_slot, 2)),
            dma((n_slot - 1, 4)),
            dma((n_slot - 1, 4)),
            dma((1,)),
            dma((n_slot,)),
        ],
        compiler_params=pltpu.CompilerParams(collective_id=0, has_side_effects=True, vmem_limit_bytes=64000000),
        name="both_passes",
    )(scal, x_loc, vt_loc)


def solution(mesh):
    def local_program(x_loc, v_loc, length_scale, out_scale):
        ell, scale = length_scale[0], out_scale[0]
        shrink = jnp.where(ell > 2.0**64, 2.0**-70, jnp.where(ell > 2.0**32, 2.0**-32, 1.0)).astype(F32)
        ell = ell * shrink
        scal = jnp.stack([LOG2E / (2.0 * ell * ell), scale, shrink * shrink])
        return both_passes(mesh.shape["row"], scal, x_loc, v_loc.T).T

    row_spec = P(("task", "row"), None)
    return jax.shard_map(local_program, mesh=mesh, in_specs=(row_spec, row_spec, P("task"), P("task")), out_specs=row_spec, check_vma=False)
```

time: 993 us -> 164 us (0.17)
  waiting for transfers between devices: 663 us -> 0 us
  matrix products: 278 us -> 0 us
  Pallas kernels: 0 us -> 160 us
  other arithmetic: 18.4 us -> 0.58 us
  starting transfers between devices: 15.9 us -> 0 us
    ppermute x124 -> x0, waiting for transfers between devices: 663 us -> none  [the longest x62 663 us: visit_step(): v_vis = lax.ppermute(v_vis, 'row', shift_pairs)]
    dot_general x65 -> x0, matrix products: 278 us -> none  [the longest x64 273 us: kernel_product(): return jnp.dot(kern_tile, v_cols, preferred_element_type=jnp.float32)]
    pallas_call x0 -> x1, Pallas kernels: none -> 160 us  [both_passes(): pl.pallas_call(kernel, in_specs=[pl.BlockSpec(memory_space=pltpu.SMEM), p...]
    reduce_sum x63 -> x0, other arithmetic: 18.4 us -> none  [the longest x62 17.1 us: visit_step(): norm_vis = jnp.sum(jnp.square(x_vis.astype(jnp.float32)), axis=1)]
    ppermute x124 -> x0, starting transfers between devices: 15.9 us -> none  [the longest x62 9.34 us: visit_step(): x_vis = lax.ppermute(x_vis, 'row', shift_pairs)]
  transfers between devices with their start and end apart: 124 -> 0, of which waited for: 62 -> 0; matrix products, arithmetic and copies ran while one was open for 0% -> 0% of each run, Pallas kernels for 0% -> 0%
where the time goes in v2:
time: 164 us; the launch traced here: 163 us
  Pallas kernels  160 us (98%)
    pallas_call x1, Pallas kernels, both_passes(): pl.pallas_call(kernel, in_specs=[pl.BlockSpec(memory_space=pltpu.SMEM), p...  160 us

profile of v2, /device:TPU:97, one launch (start us, length us, event | category | flops | bytes accessed | tf_op | source)
XLA Modules:
  0.0 163.4 jit_solution(10549517672996070466)
XLA Ops:
  1.3 0.6 pad_maximum_fusion.scal_ref
  1.9 159.9 %both_passes.1 = f32[16,1536]{1,0:T(8,128)} custom-call(f32[3]{0:T(128)} %pad_maximum_fusion.scal_ref, bf16[1536,128]{1,0:T(8,128)(2,1)} %x_ref.1, bf16[16,1536]{1,0:T(8,128)(2,1)} %bitcast.9), custom_call_target="tpu_custom_call" | custom-call | tf_op jit(solution)/shard_map/both_passes/pallas_call | solution.py:223
  161.8 1.5 copy.8

commit v3 on v2

--- a/solution.py
+++ b/solution.py
@@ -13,6 +13,7 @@
 TILE = 512
 LANES = 128
 LAG = 1
+PAD = 128
 STEP = ((1, 0), (0, 1), (-1, 0), (0, -1))
 WAVES = (
     (0, 0, 1, 0),
@@ -137,7 +138,7 @@
                 abuf[which, slot, pl.ds(lane, LANES), :] = full.T.astype(BF16)
 
         def block(buf, which, slot, first):
-            gram = {}
+            gram, part = {}, None
             if first:
                 widen(which, slot, 0)
             for u in range(n_u + LAG):
@@ -151,8 +152,11 @@
                 if u >= LAG:
                     c, r = units[u - LAG]
                     tile = jnp.minimum((jnp.exp2(gram.pop(u - LAG) * coef) * scale).astype(BF16), cap)
-                    lhs = buf[which, slot + 1, pl.ds(0, 16), pl.ds(r * TILE, TILE)]
-                    total[:, pl.ds(c * TILE, TILE)] += jnp.dot(lhs, tile, preferred_element_type=F32)
+                    rhs_rows = buf[which, slot + 1, pl.ds(0, 16), pl.ds(r * TILE, TILE)]
+                    prod = jnp.dot(jnp.concatenate([rhs_rows] * (PAD // 16), axis=0), tile, preferred_element_type=F32)
+                    part = prod if r == 0 else part + prod
+                    if r == n_r - 1:
+                        total[:, pl.ds(c * TILE, TILE)] += part
 
         total[...] = jnp.zeros_like(total)
         pl.semaphore_wait(barrier, n_slot)
@@ -184,7 +188,7 @@
             return carry
 
         lax.fori_loop(0, n_slot, first_step, 0)
-        ybuf[0, 1] = total[...].astype(BF16)
+        ybuf[0, 1] = total[pl.ds(0, 16), :].astype(BF16)
         total[...] = jnp.zeros_like(total)
         for copy in sibling_copies(n_slot - 1):
             copy.wait_send()
@@ -209,7 +213,7 @@
             return carry
 
         lax.fori_loop(0, n_slot, second_step, 0)
-        out_ref[...] = total[...]
+        out_ref[...] = total[pl.ds(0, 16), :]
         y_sibling_copy(n_slot - 1).wait_send()
 
     return kernel, n_slot
@@ -231,7 +235,7 @@
             pltpu.VMEM((2, n_slot + 1, 32, own), BF16),
             pltpu.VMEM((2, n_slot + 1, n_col, own), BF16),
             pltpu.VMEM((2 * feat, own), BF16),
-            pltpu.VMEM((n_col, own), F32),
+            pltpu.VMEM((PAD, own), F32),
             dma((2,)),
             dma((AHEAD, 4, 2)),
             dma((n_slot - 1, 4, 2)),

time: 164 us -> 158 us (0.963)
  Pallas kernels: 160 us -> 155 us
    pallas_call x1, Pallas kernels: 160 us -> 155 us  [both_passes(): pl.pallas_call(kernel, in_specs=[pl.BlockSpec(memory_space=pltpu.SMEM), p...]
where the time goes in v3:
time: 158 us
  Pallas kernels  155 us (98%)
    pallas_call x1, Pallas kernels, both_passes(): pl.pallas_call(kernel, in_specs=[pl.BlockSpec(memory_space=pltpu.SMEM), p...  155 us

profile of v3, /device:TPU:97, one launch (start us, length us, event | category | flops | bytes accessed | tf_op | source)
XLA Modules:
  0.0 158.1 jit_solution(14847999244998891639)
XLA Ops:
  1.3 0.6 pad_maximum_fusion.scal_ref
  1.9 154.6 %both_passes.1 = f32[16,1536]{1,0:T(8,128)} custom-call(f32[3]{0:T(128)} %pad_maximum_fusion.scal_ref, bf16[1536,128]{1,0:T(8,128)(2,1)} %x_ref.1, bf16[16,1536]{1,0:T(8,128)(2,1)} %bitcast.9), custom_call_target="tpu_custom_call" | custom-call | tf_op jit(solution)/shard_map/both_passes/pallas_call | solution.py:227
  156.5 1.5 copy.8

commit v4 on v3

--- a/solution.py
+++ b/solution.py
@@ -33,6 +33,8 @@
     (3, 11, 2, 2),
 )
 AHEAD = 4
+RING = 3
+KEPT_SLOTS = 3
 
 
 def split3(val):
@@ -47,12 +49,13 @@
     n_slot = side * side
     quarter = own // 4
     n_c, n_r = own // TILE, own // TILE
+    n_far = 2 * (n_slot - KEPT_SLOTS)
     units = [(c, r) for c in range(n_c) for r in range(n_r)]
     n_u = len(units)
 
     def kernel(
-        scal_ref, x_ref, vt_ref, out_ref, xbuf, abuf, vbuf, ybuf, wbuf, total,
-        load_sem, send_sem, recv_sem, sib_send, sib_recv, ysend_sem, yrecv_sem, ysib_send, ysib_recv,
+        scal_ref, x_ref, vt_ref, out_ref, store_ref, xbuf, abuf, vbuf, ybuf, wbuf, total, tbuf,
+        load_sem, send_sem, recv_sem, sib_send, sib_recv, ysend_sem, yrecv_sem, ysib_send, ysib_recv, spill_sem, fetch_sem,
     ):
         me = lax.axis_index("row")
         core, chip = me % 2, me // 2
@@ -64,7 +67,7 @@
         sibling = {"row": chip * 2 + 1 - core}
 
         load_x = pltpu.make_async_copy(x_ref, xbuf.at[0, 0], load_sem.at[0])
-        load_v = pltpu.make_async_copy(vt_ref, vbuf.at[0, 1, pl.ds(0, 16)], load_sem.at[1])
+        load_v = pltpu.make_async_copy(vt_ref, vbuf.at[0, 0, pl.ds(0, 16)], load_sem.at[1])
         load_x.start()
         load_v.start()
 
@@ -89,7 +92,7 @@
             for i, part in enumerate(parts):
                 vis = jnp.where(row_idx == i, part, vis)
                 mine = jnp.where(row_idx == i + 3, -part, mine)
-            vbuf[0, 1, pl.ds(16, 16), pl.ds(r * LANES, LANES)] = vis.astype(BF16)
+            vbuf[0, 0, pl.ds(16, 16), pl.ds(r * LANES, LANES)] = vis.astype(BF16)
             wbuf[pl.ds(0, LANES), pl.ds(r * LANES, LANES)] = (x_t * (2.0 * shrink2)).astype(BF16)
             wbuf[pl.ds(LANES, 16), pl.ds(r * LANES, LANES)] = mine.astype(BF16)
 
@@ -103,7 +106,7 @@
                 copies.append(pltpu.make_async_remote_copy(
                     xbuf.at[0, src, rows], xbuf.at[0, wave + 1, rows], send_sem.at[wave % AHEAD, q, 0], recv_sem.at[wave, q, 0], device_id=target))
                 copies.append(pltpu.make_async_remote_copy(
-                    vbuf.at[0, src + 1, :, rows], vbuf.at[0, wave + 2, :, rows], send_sem.at[wave % AHEAD, q, 1], recv_sem.at[wave, q, 1], device_id=target))
+                    vbuf.at[0, src, :, rows], vbuf.at[0, wave + 1, :, rows], send_sem.at[wave % AHEAD, q, 1], recv_sem.at[wave, q, 1], device_id=target))
             return copies
 
         def piece_copies(slot):
@@ -114,49 +117,72 @@
                 copies.append(pltpu.make_async_remote_copy(
                     xbuf.at[0, slot, rows], xbuf.at[0, slot, rows], send_sem.at[sem, q, 0], recv_sem.at[slot - 1, q, 0], device_id=sibling))
                 copies.append(pltpu.make_async_remote_copy(
-                    vbuf.at[0, slot + 1, :, rows], vbuf.at[0, slot + 1, :, rows], send_sem.at[sem, q, 1], recv_sem.at[slot - 1, q, 1], device_id=sibling))
+                    vbuf.at[0, slot, :, rows], vbuf.at[0, slot, :, rows], send_sem.at[sem, q, 1], recv_sem.at[slot - 1, q, 1], device_id=sibling))
             return copies
 
         def sibling_copies(slot):
             return (
                 pltpu.make_async_remote_copy(xbuf.at[0, slot], xbuf.at[1, slot], sib_send.at[0], sib_recv.at[slot, 0], device_id=sibling),
-                pltpu.make_async_remote_copy(vbuf.at[0, slot + 1], vbuf.at[1, slot + 1], sib_send.at[1], sib_recv.at[slot, 1], device_id=sibling),
+                pltpu.make_async_remote_copy(vbuf.at[0, slot], vbuf.at[1, slot], sib_send.at[1], sib_recv.at[slot, 1], device_id=sibling),
             )
 
         def y_piece_copy(slot, q, target):
             rows = pl.ds(q * quarter, quarter)
             return pltpu.make_async_remote_copy(
-                ybuf.at[0, 1, :, rows], ybuf.at[0, slot + 1, :, rows], ysend_sem.at[slot - 1, q], yrecv_sem.at[slot - 1, q], device_id=target)
-
-        def y_sibling_copy(slot):
-            return pltpu.make_async_remote_copy(ybuf.at[0, slot + 1], ybuf.at[1, slot + 1], ysib_send.at[0], ysib_recv.at[slot], device_id=sibling)
+                ybuf.at[0, 0, :, rows], ybuf.at[0, slot, :, rows], ysend_sem.at[slot - 1, q], yrecv_sem.at[slot - 1, q], device_id=target)
+
+        def y_sibling_copy(slot, chain):
+            return pltpu.make_async_remote_copy(ybuf.at[0, slot], ybuf.at[1, slot], ysib_send.at[chain], ysib_recv.at[slot], device_id=sibling)
+
+        def spill(idx):
+            return pltpu.make_async_copy(tbuf.at[idx % RING], store_ref.at[idx], spill_sem.at[idx % RING])
+
+        def fetch(idx):
+            return pltpu.make_async_copy(store_ref.at[idx], tbuf.at[idx % RING], fetch_sem.at[idx % RING])
 
         def widen(which, slot, r):
             for lane in range(r * TILE, (r + 1) * TILE, LANES):
-                rows = vbuf[which, slot + 1, pl.ds(16, 16), pl.ds(lane, LANES)].astype(F32)
+                rows = vbuf[which, slot, pl.ds(16, 16), pl.ds(lane, LANES)].astype(F32)
                 full = jnp.concatenate([rows, jnp.zeros((LANES - 16, LANES), F32)], axis=0)
-                abuf[which, slot, pl.ds(lane, LANES), :] = full.T.astype(BF16)
-
-        def block(buf, which, slot, first):
+                abuf[which, pl.ds(lane, LANES), :] = full.T.astype(BF16)
+
+        def first_block(which, slot):
+            idx = 2 * slot + which
+            kept = idx // n_far
+            place = (idx % RING) * (1 - kept) + (idx - n_far + RING) * kept
+
+            @pl.when((idx >= RING) & (idx < n_far))
+            def _():
+                spill(idx - RING).wait()
+
             gram, part = {}, None
-            if first:
-                widen(which, slot, 0)
+            widen(which, slot, 0)
             for u in range(n_u + LAG):
-                if first and u + 1 < n_r:
+                if u + 1 < n_r:
                     widen(which, slot, u + 1)
                 if u < n_u:
                     c, r = units[u]
                     rows = pl.ds(r * TILE, TILE)
-                    lhs = jnp.concatenate([xbuf[which, slot, rows, :], abuf[which, slot, rows, :]], axis=1)
+                    lhs = jnp.concatenate([xbuf[which, slot, rows, :], abuf[which, rows, :]], axis=1)
                     gram[u] = jnp.dot(lhs, wbuf[:, pl.ds(c * TILE, TILE)], preferred_element_type=F32)
                 if u >= LAG:
                     c, r = units[u - LAG]
                     tile = jnp.minimum((jnp.exp2(gram.pop(u - LAG) * coef) * scale).astype(BF16), cap)
-                    rhs_rows = buf[which, slot + 1, pl.ds(0, 16), pl.ds(r * TILE, TILE)]
-                    prod = jnp.dot(jnp.concatenate([rhs_rows] * (PAD // 16), axis=0), tile, preferred_element_type=F32)
+                    tbuf[place, pl.ds(r * TILE, TILE), pl.ds(c * TILE, TILE)] = tile
+                    v_rows = vbuf[which, slot, pl.ds(0, 16), pl.ds(r * TILE, TILE)]
+                    prod = jnp.dot(jnp.concatenate([v_rows] * (PAD // 16), axis=0), tile, preferred_element_type=F32)
                     part = prod if r == 0 else part + prod
                     if r == n_r - 1:
                         total[:, pl.ds(c * TILE, TILE)] += part
+
+            @pl.when(idx < n_far)
+            def _():
+                spill(idx).start()
+
+        def second_block(place, which, slot):
+            for c in range(n_c):
+                cols = pl.ds(c * TILE, TILE)
+                total[pl.ds(0, 16), cols] += jnp.dot(ybuf[which, slot], tbuf[place, :, cols], preferred_element_type=F32)
 
         total[...] = jnp.zeros_like(total)
         pl.semaphore_wait(barrier, n_slot)
@@ -181,40 +207,75 @@
                     for copy in wave_copies(wave):
                         copy.start()
 
-            block(vbuf, 0, slot, True)
+            @pl.when(slot == n_slot - KEPT_SLOTS)
+            def _():
+                for idx in range(RING):
+                    spill(n_far - RING + idx).wait()
+                for idx in range(RING):
+                    fetch(idx).start()
+
+            first_block(0, slot)
             for copy in sibling_copies(slot):
                 copy.wait_recv()
-            block(vbuf, 1, slot, True)
+            first_block(1, slot)
             return carry
 
         lax.fori_loop(0, n_slot, first_step, 0)
-        ybuf[0, 1] = total[pl.ds(0, 16), :].astype(BF16)
+        ybuf[0, 0] = total[pl.ds(0, 16), :].astype(BF16)
         total[...] = jnp.zeros_like(total)
         for copy in sibling_copies(n_slot - 1):
             copy.wait_send()
 
-        y_sibling_copy(0).start()
+        y_sibling_copy(0, 0).start()
         for wave, (_, _, prim, sec) in enumerate(WAVES):
             for q in range(4):
                 (px, py), (sx, sy) = STEP[q], STEP[(q + 1) % 4]
                 y_piece_copy(wave + 1, q, chip_id((prim * px + sec * sx) % side, (prim * py + sec * sy) % side)).start()
 
+        n_far_slots = n_slot - KEPT_SLOTS
+
+        def far_block(which, slot):
+            idx = 2 * slot + which
+            fetch(idx).wait()
+            second_block(idx % RING, which, slot)
+
+            @pl.when(idx + RING < n_far)
+            def _():
+                fetch(idx + RING).start()
+
+        def pass_on(slot, chain):
+            for q in range(4):
+                y_piece_copy(slot, q, sibling).wait()
+            y_sibling_copy(slot, chain).start()
+
         def second_step(slot, carry):
             @pl.when(slot > 0)
             def _():
-                for q in range(4):
-                    y_piece_copy(slot, q, sibling).wait()
-                y_sibling_copy(slot).wait_send()
-                y_sibling_copy(slot).start()
-
-            block(ybuf, 0, slot, False)
-            y_sibling_copy(slot).wait_recv()
-            block(ybuf, 1, slot, False)
+                y_sibling_copy(slot, 0).wait_send()
+                pass_on(slot, 0)
+
+            far_block(0, slot)
+            y_sibling_copy(slot, 0).wait_recv()
+            far_block(1, slot)
+            near = slot - (n_far_slots - 2 * KEPT_SLOTS)
+            near_slot = n_far_slots + near // 2
+
+            @pl.when((near >= 0) & (near % 2 == 0))
+            def _():
+                pass_on(near_slot, 1)
+                second_block(RING + near, 0, near_slot)
+
+            @pl.when((near >= 0) & (near % 2 == 1))
+            def _():
+                y_sibling_copy(near_slot, 1).wait_send()
+                y_sibling_copy(near_slot, 1).wait_recv()
+                second_block(RING + near, 1, near_slot)
+
             return carry
 
-        lax.fori_loop(0, n_slot, second_step, 0)
+        lax.fori_loop(0, n_far_slots, second_step, 0)
         out_ref[...] = total[pl.ds(0, 16), :]
-        y_sibling_copy(n_slot - 1).wait_send()
+        y_sibling_copy(n_far_slots - 1, 0).wait_send()
 
     return kernel, n_slot
 
@@ -227,15 +288,16 @@
     return pl.pallas_call(
         kernel,
         in_specs=[pl.BlockSpec(memory_space=pltpu.SMEM), pl.BlockSpec(memory_space=pl.ANY), pl.BlockSpec(memory_space=pl.ANY)],
-        out_specs=pl.BlockSpec(memory_space=pltpu.VMEM),
-        out_shape=jax.ShapeDtypeStruct((n_col, own), F32),
+        out_specs=[pl.BlockSpec(memory_space=pltpu.VMEM), pl.BlockSpec(memory_space=pl.ANY)],
+        out_shape=[jax.ShapeDtypeStruct((n_col, own), F32), jax.ShapeDtypeStruct((2 * (n_slot - KEPT_SLOTS), own, own), BF16)],
         scratch_shapes=[
             pltpu.VMEM((2, n_slot, own, feat), BF16),
-            pltpu.VMEM((2, n_slot, own, feat), BF16),
-            pltpu.VMEM((2, n_slot + 1, 32, own), BF16),
-            pltpu.VMEM((2, n_slot + 1, n_col, own), BF16),
+            pltpu.VMEM((2, own, feat), BF16),
+            pltpu.VMEM((2, n_slot, 32, own), BF16),
+            pltpu.VMEM((2, n_slot, n_col, own), BF16),
             pltpu.VMEM((2 * feat, own), BF16),
             pltpu.VMEM((PAD, own), F32),
+            pltpu.VMEM((RING + 2 * KEPT_SLOTS, own, own), BF16),
             dma((2,)),
             dma((AHEAD, 4, 2)),
             dma((n_slot - 1, 4, 2)),
@@ -243,12 +305,14 @@
             dma((n_slot, 2)),
             dma((n_slot - 1, 4)),
             dma((n_slot - 1, 4)),
-            dma((1,)),
+            dma((2,)),
             dma((n_slot,)),
+            dma((RING,)),
+            dma((RING,)),
         ],
-        compiler_params=pltpu.CompilerParams(collective_id=0, has_side_effects=True, vmem_limit_bytes=64000000),
+        compiler_params=pltpu.CompilerParams(collective_id=0, has_side_effects=True, vmem_limit_bytes=67000000),
         name="both_passes",
-    )(scal, x_loc, vt_loc)
+    )(scal, x_loc, vt_loc)[0]
 
 
 def solution(mesh):

time: 158 us -> 133 us (0.84)
  Pallas kernels: 155 us -> 129 us
    pallas_call x1, Pallas kernels: 155 us -> 129 us  [both_passes(): pl.pallas_call(kernel, in_specs=[pl.BlockSpec(memory_space=pltpu.SMEM), p...]
where the time goes in v4:
time: 133 us
  Pallas kernels  129 us (97%)
  local copies, waits for them, and re-layouts  1.54 us (1%)
  between operations  1.36 us (1%)
    pallas_call x1, Pallas kernels, both_passes(): pl.pallas_call(kernel, in_specs=[pl.BlockSpec(memory_space=pltpu.SMEM), p...  129 us

profile of v4, /device:TPU:97, one launch (start us, length us, event | category | flops | bytes accessed | tf_op | source)
XLA Modules:
  0.0 132.6 jit_solution(11206861418329455156)
XLA Ops:
  1.3 0.7 pad_maximum_fusion.scal_ref
  2.0 129.0 %both_passes.1 = (f32[16,1536]{1,0:T(8,128)}, bf16[26,1536,1536]{2,1,0:T(8,128)(2,1)}) custom-call(f32[3]{0:T(128)} %pad_maximum_fusion.scal_ref, bf16[1536,128]{1,0:T(8,128)(2,1)} %x_ref.1, bf16[16,1536]{1,0:T(8,128)(2,1)} %bitcast.9), custom_call_target="tpu_custom_call" | custom-call | tf_op jit(solution)/shard_map/both_passes/pallas_call | solution.py:288
  131.0 1.5 %copy.8 = f32[1536,16]{0,1:T(8,128)} copy(f32[1536,16]{0,1:T(8,128)} %bitcast.8) | data formatting | bytes 196608
